TPU v7x, 256 devices: a whole 4x4x8 slice. The times are simulated.
256 devices in a mesh: branch: 64 (over z, x, core), col: 4 (over y).
Axes of the slice: x: 4, y: 4, z: 8, core: 2. Of those that a mesh axis runs over, the one named last changes fastest.
Arguments:
- vectors: bfloat16 [128, 524288], P('col', 'branch'), may hold values from -6 to 6
- basis: bfloat16 [2, 2048, 64, 256], P(None, 'branch'), may hold values from -0.375 to 0.375
- leaf_transfer: bfloat16 [2, 64, 131072], P(None, None, 'branch'), may hold values from -0.125 to 0.125
- upper_transfer: bfloat16 [2, 4, 64, 128], replicated, may hold values from -0.5 to 0.5
- upper_coupling: bfloat16 [2, 5, 64, 256], replicated, may hold values from -0.4375 to 0.4375
- leaf_coupling: bfloat16 [2, 2048, 64, 512], P(None, 'branch'), may hold values from -0.375 to 0.375
- near_blocks: bfloat16 [2, 2048, 4, 256, 256], P(None, 'branch'), may hold values from -0.25 to 0.25
- far_mask: int32 [5, 64, 4], replicated, may hold values 0 or 1
- far_ids: int32 [2048, 8], P('branch'), may hold values from 0 to 2047, as said below
- far_count: int32 [2048], P('branch'), may hold values from 1 to 8
- near_ids: int32 [2048, 4], P('branch'), may hold values from 0 to 2047, as said below
- near_count: int32 [2048], P('branch'), may hold values from 2 to 4, as said below
Outputs:
- sample: bfloat16 [128, 524288], P('col', 'branch')
Inputs may be any that keep to these rules, and one draw needn't show every extreme that they name: `near_ids`: entry 0 of leaf i's list is i itself; every entry lies between (i // 32 - 1) * 32 and (i // 32 + 2) * 32 - 1. `far_ids`: every entry of leaf i's list lies between (i // 32 - 1) * 32 and (i // 32 + 2) * 32 - 1. `near_count`: some leaf has 4 live slots.
All inputs are finite; a program needn't handle non-finite values.
Results may differ from a plain program's by a relative error of at most 0.014.
Values may be sent and summed in bfloat16 or wider, within the bound.
A program may use at most 128 MiB of HBM per device.

v0:
```python
import jax
import jax.numpy as jnp
from jax import lax
from jax.sharding import PartitionSpec as P

OFFSETS = (-3, -2, 2, 3)


def joined_along(blocks, dim):
    lengths = list(blocks.shape[1:])
    lengths[dim] *= blocks.shape[0]
    return jnp.moveaxis(blocks, 0, dim).reshape(lengths)


def from_everyone(value, axis):
    length = lax.axis_size(axis)
    return lax.all_to_all(
        jnp.broadcast_to(value[None], (length, *value.shape)), axis, 0, 0, tiled=True
    )


def gathered_copies(value, axis, dim):
    return joined_along(from_everyone(value, axis), dim)


def padded_2(cells, sides, width):
    for axis, dim in sides:
        count = lax.axis_size(axis)
        ends = count - 1
        head = lax.slice_in_dim(cells, 0, width, axis=dim)
        tail = lax.slice_in_dim(cells, cells.shape[dim] - width, cells.shape[dim], axis=dim)
        cells = jnp.concatenate(
            [
                lax.ppermute(tail, axis, [(i, (i + 1) % count) for i in range(ends)]),
                cells,
                lax.ppermute(head, axis, [((i + 1) % count, i) for i in range(ends)]),
            ],
            axis=dim,
        )
    return cells


def pick_rows(source, leaf_index, live_count):
    picked = jnp.take(source, leaf_index.reshape(-1), axis=1)
    picked = picked.reshape(
        source.shape[0], leaf_index.shape[0], leaf_index.shape[1], source.shape[2]
    )
    active = lax.broadcasted_iota(jnp.int32, leaf_index.shape, 1) < live_count[:, None]
    return jnp.where(active[None, :, :, None], picked, jnp.zeros((), source.dtype))


def near_product(dense_blocks, source, leaf_index, live_count):
    picked = pick_rows(source, leaf_index, live_count)
    return jnp.einsum("ijrc,vijc->vir", dense_blocks, picked, preferred_element_type=jnp.float32)


def tree_gathered(box_coef, upper_transfer, upper_coupling, far_mask, matrix_index, device_index):
    lifts = upper_coupling.shape[1]
    rank_size = box_coef.shape[1]
    every_node = gathered_copies(box_coef[None], "branch", 0)
    lifted = [every_node]
    for height in range(lifts - 1):
        below = lifted[-1]
        siblings = jnp.concatenate([below[0::2], below[1::2]], axis=2)
        lifted.append(
            jnp.einsum(
                "nvj,kj->nvk",
                siblings,
                upper_transfer[matrix_index, height],
                preferred_element_type=jnp.float32,
            ).astype(jnp.bfloat16)
        )
    descent = None
    for height in reversed(range(lifts)):
        current = lifted[height]
        nodes = current.shape[0]
        padded = jnp.pad(current, ((3, 3), (0, 0), (0, 0)))
        stacked = jnp.concatenate(
            [padded[3 + offset : 3 + offset + nodes] for offset in OFFSETS], axis=2
        )
        active = jnp.repeat(far_mask[height, :nodes], rank_size, axis=1) > 0
        stacked = jnp.where(active[:, None, :], stacked, jnp.zeros((), jnp.bfloat16))
        coupled = jnp.einsum(
            "nvj,kj->nvk",
            stacked,
            upper_coupling[matrix_index, height],
            preferred_element_type=jnp.float32,
        )
        if descent is not None:
            joined = upper_transfer[matrix_index, height].reshape(rank_size, 2, rank_size)
            child = jnp.einsum(
                "ksj,nvk->nsvj",
                joined,
                descent.astype(jnp.bfloat16),
                preferred_element_type=jnp.float32,
            )
            coupled = coupled + child.reshape(nodes, -1, rank_size)
        descent = coupled
    return lax.dynamic_index_in_dim(descent, device_index, 0, keepdims=False)


def apply_matrix(
    matrix_index,
    vectors,
    basis,
    leaf_transfer,
    upper_transfer,
    upper_coupling,
    leaf_coupling,
    near_blocks,
    far_mask,
    far_ids,
    far_count,
    near_ids,
    near_count,
):
    columns = vectors.shape[0]
    per_device = basis.shape[1]
    rank_size = basis.shape[2]
    leaf_size = basis.shape[3]
    device_index = lax.axis_index("branch")
    leaf_rows = vectors.reshape(columns, per_device, leaf_size)
    leaf_coef = jnp.einsum(
        "ikr,vir->vik", basis[matrix_index], leaf_rows, preferred_element_type=jnp.float32
    ).astype(jnp.bfloat16)
    flat_coef = leaf_coef.reshape(columns, per_device * rank_size)
    box_coef = jnp.einsum(
        "vj,kj->vk", flat_coef, leaf_transfer[matrix_index], preferred_element_type=jnp.float32
    ).astype(jnp.bfloat16)
    descent = tree_gathered(
        box_coef, upper_transfer, upper_coupling, far_mask, matrix_index, device_index
    )
    parent = descent.astype(jnp.bfloat16)
    from_tree = jnp.dot(
        parent, leaf_transfer[matrix_index], preferred_element_type=jnp.float32
    ).reshape(columns, per_device, rank_size)
    first_leaf = (device_index - 1) * per_device
    coef_halo = padded_2(leaf_coef, (("branch", 1),), per_device)
    picked = pick_rows(coef_halo, far_ids - first_leaf, far_count).reshape(columns, per_device, -1)
    leaf_field = (
        jnp.einsum(
            "ikj,vij->vik", leaf_coupling[matrix_index], picked, preferred_element_type=jnp.float32
        )
        + from_tree
    )
    leaf_round = leaf_field.astype(jnp.bfloat16)
    far_terms = jnp.einsum(
        "ikr,vik->vir", basis[matrix_index], leaf_round, preferred_element_type=jnp.float32
    )
    vector_halo = padded_2(leaf_rows, (("branch", 1),), per_device)
    local_index = near_ids - first_leaf
    near_terms = near_product(near_blocks[matrix_index], vector_halo, local_index, near_count)
    return (near_terms + far_terms).astype(jnp.bfloat16).reshape(columns, per_device * leaf_size)


def shards(
    vectors,
    basis,
    leaf_transfer,
    upper_transfer,
    upper_coupling,
    leaf_coupling,
    near_blocks,
    far_mask,
    far_ids,
    far_count,
    near_ids,
    near_count,
):
    first = apply_matrix(
        0,
        vectors,
        basis,
        leaf_transfer,
        upper_transfer,
        upper_coupling,
        leaf_coupling,
        near_blocks,
        far_mask,
        far_ids,
        far_count,
        near_ids,
        near_count,
    )
    return apply_matrix(
        1,
        first,
        basis,
        leaf_transfer,
        upper_transfer,
        upper_coupling,
        leaf_coupling,
        near_blocks,
        far_mask,
        far_ids,
        far_count,
        near_ids,
        near_count,
    )


def solution(mesh):
    return jax.shard_map(
        shards,
        mesh=mesh,
        in_specs=(
            P("col", "branch"),
            P(None, "branch", None, None),
            P(None, None, "branch"),
            P(),
            P(),
            P(None, "branch", None, None),
            P(None, "branch", None, None, None),
            P(),
            P("branch", None),
            P("branch"),
            P("branch", None),
            P("branch"),
        ),
        out_specs=P("col", "branch"),
        check_vma=False,
    )
```

profile of v0, /device:TPU:1, one launch (start us, length us, event | category | flops | bytes accessed | tf_op | source)
XLA Modules:
  0.0 169.9 jit_solution(11999364993784570683)
XLA Ops:
  0.0 1.9 %fusion.78 = bf16[32,32,64]{2,0,1:T(8,128)(2,1)S(1)} fusion(bf16[2,32,64,256]{3,2,1,0:T(8,128)(2,1)} %param.17, bf16[4,32,8,256]{3,2,1,0:T(8,128)(2,1)} %bitcast.369), kind=kOutput, calls=%fused_computation.52 | convolution fusion | flops 33619968 | bytes 1703936 | tf_op jit(solution)/shard_map/ikr,vir->vik/dot_general | solution.py:123
  1.9 5.1 %collective-permute-start.3 = (bf16[32,32,64]{2,0,1:T(8,128)(2,1)S(1)}, bf16[32,32,64]{2,0,1:T(8,128)(2,1)S(1)}, u32[]{:S(2)}, u32[]{:S(2)}) collective-permute-start(bf16[32,32,64]{2,0,1:T(8,128)(2,1)S(1)} %fusion.78), channel_id=1, source_target_pairs={{4,0},{8,4},{12,8},{16,12},{20,16},{24,20},{28,24},{32,28},{36,32}... | collective-permute-start | bytes 393224 | tf_op jit(solution)/shard_map/ppermute | solution.py:36
  7.0 1.9 %collective-permute-start.2 = (bf16[32,32,64]{2,0,1:T(8,128)(2,1)S(1)}, bf16[32,32,64]{2,0,1:T(8,128)(2,1)S(1)}, u32[]{:S(2)}, u32[]{:S(2)}) collective-permute-start(bf16[32,32,64]{2,0,1:T(8,128)(2,1)S(1)} %fusion.78), channel_id=1, source_target_pairs={{0,4},{4,8},{8,12},{12,16},{16,20},{20,24},{24,28},{28,32},{32,36}... | collective-permute-start | bytes 393224 | tf_op jit(solution)/shard_map/ppermute | solution.py:34
  9.8 2.6 %collective-permute-start.1 = (bf16[32,32,256]{2,0,1:T(8,128)(2,1)}, bf16[32,32,256]{2,0,1:T(8,128)(2,1)}, u32[]{:S(2)}, u32[]{:S(2)}) collective-permute-start(bf16[32,32,256]{2,0,1:T(8,128)(2,1)} %bitcast.360), channel_id=1, source_target_pairs={{4,0},{8,4},{12,8},{16,12},{20,16},{24,20},{28,24},{32,28},{36,32}... | collective-permute-start | bytes 1572872 | tf_op jit(solution)/shard_map/ppermute | solution.py:36
  12.4 3.1 %collective-permute-start = (bf16[32,32,256]{2,0,1:T(8,128)(2,1)}, bf16[32,32,256]{2,0,1:T(8,128)(2,1)}, u32[]{:S(2)}, u32[]{:S(2)}) collective-permute-start(bf16[32,32,256]{2,0,1:T(8,128)(2,1)} %bitcast.360), channel_id=1, source_target_pairs={{0,4},{4,8},{8,12},{12,16},{16,20},{20,24},{24,28},{28,32},{32,36}... | collective-permute-start | bytes 1572872 | tf_op jit(solution)/shard_map/ppermute | solution.py:34
  17.2 14.9 %all-to-all-start = ((bf16[64,2,1024]{2,1,0:T(2,128)(2,1)}), bf16[64,2,1024]{2,1,0:T(2,128)(2,1)S(1)}, u32[]{:S(2)}, u32[]{:S(2)}) async-start(bf16[64,2,1024]{2,1,0:T(2,128)(2,1)} %reshape.283), calls=%async_computation | async-start | bytes 524288 | tf_op jit(solution)/shard_map/all_to_all | solution.py:17
  56.5 2.6 %fusion.96 = f32[64,32,64]{2,1,0:T(8,128)} fusion(bf16[64,32,64]{2,1,0:T(8,128)(2,1)S(1)} %get-tuple-element.16, bf16[64,32,64]{2,1,0:T(8,128)(2,1)S(1)} %get-tuple-element.15, bf16[64,32,64]{2,1,0:T(8,128)(2,1)S(1)} %get-tuple-element.14, bf16[64,32,64]{2,1,0:T(8,128)(2,1)S(1)} %get-tuple-element.13, pred[64,256]{1,0:T(8,128)(4,1)S(1)} %copy-done.18, ...), kind=kOutput, calls=%fused_computation.79 | convolution fusion | flops 71827456 | bytes 1622016 | tf_op jit(solution)/shard_map/nvj,kj->nvk/dot_general | solution.py:83
  61.4 2.0 %fusion.128 = f32[16,32,2,64]{3,1,2,0:T(8,128)} fusion(f32[16,32,64]{2,1,0:T(8,128)S(1)} %bitcast.377, bf16[16,32,64]{2,1,0:T(8,128)(2,1)S(1)} %get-tuple-element.50, bf16[16,32,64]{2,1,0:T(8,128)(2,1)S(1)} %get-tuple-element.49, bf16[16,32,64]{2,1,0:T(8,128)(2,1)S(1)} %get-tuple-element.48, bf16[16,32,64]{2,1,0:T(8,128)(2,1)S(1)} %get-tuple-element.47, ...), kind=kOutput, calls=%fused_computation.114 | convolution fusion | flops 26411008 | bytes 708608 | tf_op jit(solution)/shard_map/ksj,nvk->nsvj/dot_general | solution.py:91
  63.4 3.0 %fusion.126 = f32[32,32,2,64]{3,1,2,0:T(8,128)} fusion(f32[32,32,64]{2,1,0:T(8,128)} %bitcast.375, bf16[32,32,64]{2,1,0:T(8,128)(2,1)} %get-tuple-element.30, bf16[32,32,64]{2,1,0:T(8,128)(2,1)} %get-tuple-element.29, bf16[32,32,64]{2,1,0:T(8,128)(2,1)} %get-tuple-element.28, bf16[32,32,64]{2,1,0:T(8,128)(2,1)S(1)} %get-tuple-element.27, ...), kind=kOutput, calls=%fused_computation.112 | convolution fusion | flops 52822016 | bytes 2039808 | tf_op jit(solution)/shard_map/ksj,nvk->nsvj/dot_general | solution.py:91
  66.5 2.5 %fusion.355 = f32[32,32,64]{2,0,1:T(8,128)} fusion(bf16[32,64,64]{2,1,0:T(8,128)(2,1)} %bitcast.368, f32[64,32,64]{2,1,0:T(8,128)} %bitcast.373, s32[]{:T(128)S(6)} %select_n.77, f32[64,32,64]{2,1,0:T(8,128)} %fusion.96), kind=kOutput, calls=%fused_computation.316 | convolution fusion | flops 8392704 | bytes 819204 | tf_op jit(solution)/shard_map/dot_general | solution.py:134
  68.9 3.8 %fusion.81 = f32[32,32,256]{2,1,0:T(8,128)} fusion(f32[32,32,64]{2,0,1:T(8,128)} %fusion.355, bf16[2,32,64,512]{3,2,1,0:T(8,128)(2,1)} %param.21, bf16[32,32,512]{2,1,0:T(8,128)(2,1)S(1)} %copy-done.4, bf16[2,32,64,256]{3,2,1,0:T(8,128)(2,1)S(1)} %copy-done), kind=kOutput, calls=%fused_computation.54 | convolution fusion | flops 100794368 | bytes 5767168 | tf_op jit(solution)/shard_map/ikr,vik->vir/dot_general | solution.py:147
  72.8 1.5 pad_maximum_fusion
  74.3 2.1 %gather_fusion = bf16[128,32,256]{2,1,0:T(8,128)(2,1)} fusion(bf16[32,96,256]{2,0,1:T(8,128)(2,1)S(1)} %pad_maximum_fusion, s32[1024]{0:T(1024)} %pad_clamp_fusion.1), kind=kCustom, calls=%fused_computation.clone | custom fusion | bytes 4194816 | tf_op jit(solution)/shard_map/jit(_take)/gather | solution.py:44
  76.4 3.3 %broadcast_select_fusion = bf16[128,32,256]{2,1,0:T(8,128)(2,1)} fusion(bf16[128,32,256]{2,1,0:T(8,128)(2,1)} %gather_fusion, pred[128]{0:T(512)(128)(4,1)S(1)} %copy-done.27), kind=kLoop, calls=%fused_computation.20 | loop fusion | flops 1048576 | bytes 4194432 | tf_op jit(solution)/shard_map/jit(_take)/select_n | solution.py:44
  79.7 12.3 %fusion.63 = bf16[32,32,256]{2,0,1:T(8,128)(2,1)} fusion(f32[32,32,256]{2,1,0:T(8,128)S(1)} %copy-done.6, bf16[2,32,4,256,256]{4,3,2,1,0:T(8,128)(2,1)} %param.22, bf16[32,32,4,256]{3,0,2,1:T(8,128)(2,1)} %bitcast.366, pred[32,4]{1,0:T(8,128)(4,1)S(1)} %copy-done.24), kind=kOutput, calls=%fused_computation.39 | convolution fusion | flops 538443776 | bytes 20447360 | tf_op jit(solution)/shard_map/ijrc,vijc->vir/dot_general | solution.py:54
  92.1 1.5 fusion.79
  93.7 2.4 %collective-permute-start.7 = (bf16[32,32,64]{2,0,1:T(8,128)(2,1)S(1)}, bf16[32,32,64]{2,0,1:T(8,128)(2,1)S(1)}, u32[]{:S(2)}, u32[]{:S(2)}) collective-permute-start(bf16[32,32,64]{2,0,1:T(8,128)(2,1)S(1)} %fusion.79), channel_id=1, source_target_pairs={{4,0},{8,4},{12,8},{16,12},{20,16},{24,20},{28,24},{32,28},{36,32}... | collective-permute-start | bytes 393224 | tf_op jit(solution)/shard_map/ppermute | solution.py:36
  96.1 3.2 %collective-permute-start.6 = (bf16[32,32,64]{2,0,1:T(8,128)(2,1)S(1)}, bf16[32,32,64]{2,0,1:T(8,128)(2,1)S(1)}, u32[]{:S(2)}, u32[]{:S(2)}) collective-permute-start(bf16[32,32,64]{2,0,1:T(8,128)(2,1)S(1)} %fusion.79), channel_id=1, source_target_pairs={{0,4},{4,8},{8,12},{12,16},{16,20},{20,24},{24,28},{28,32},{32,36}... | collective-permute-start | bytes 393224 | tf_op jit(solution)/shard_map/ppermute | solution.py:34
  99.3 1.9 %collective-permute-start.5 = (bf16[32,32,256]{2,0,1:T(8,128)(2,1)}, bf16[32,32,256]{2,0,1:T(8,128)(2,1)}, u32[]{:S(2)}, u32[]{:S(2)}) collective-permute-start(bf16[32,32,256]{2,0,1:T(8,128)(2,1)} %fusion.63), channel_id=1, source_target_pairs={{4,0},{8,4},{12,8},{16,12},{20,16},{24,20},{28,24},{32,28},{36,32}... | collective-permute-start | bytes 1572872 | tf_op jit(solution)/shard_map/ppermute | solution.py:36
  101.2 3.6 %collective-permute-start.4 = (bf16[32,32,256]{2,0,1:T(8,128)(2,1)}, bf16[32,32,256]{2,0,1:T(8,128)(2,1)}, u32[]{:S(2)}, u32[]{:S(2)}) collective-permute-start(bf16[32,32,256]{2,0,1:T(8,128)(2,1)} %fusion.63), channel_id=1, source_target_pairs={{0,4},{4,8},{8,12},{12,16},{16,20},{20,24},{24,28},{28,32},{32,36}... | collective-permute-start | bytes 1572872 | tf_op jit(solution)/shard_map/ppermute | solution.py:34
  106.4 14.2 %all-to-all-start.1 = ((bf16[64,2,1024]{2,1,0:T(2,128)(2,1)}), bf16[64,2,1024]{2,1,0:T(2,128)(2,1)S(1)}, u32[]{:S(2)}, u32[]{:S(2)}) async-start(bf16[64,2,1024]{2,1,0:T(2,128)(2,1)} %reshape.285), calls=%async_computation.1 | async-start | bytes 524288 | tf_op jit(solution)/shard_map/all_to_all | solution.py:17
  126.1 7.6 %all-to-all-done.1 = bf16[64,2,1024]{2,1,0:T(2,128)(2,1)S(1)} async-done(((bf16[64,2,1024]{2,1,0:T(2,128)(2,1)}), bf16[64,2,1024]{2,1,0:T(2,128)(2,1)S(1)}, u32[]{:S(2)}, u32[]{:S(2)}) %all-to-all-start.1) | async-done | bytes 262176 | tf_op jit(solution)/shard_map/all_to_all | solution.py:17
  136.7 2.6 %fusion.103 = f32[64,32,64]{2,1,0:T(8,128)} fusion(bf16[64,32,64]{2,1,0:T(8,128)(2,1)S(1)} %get-tuple-element.10, bf16[64,32,64]{2,1,0:T(8,128)(2,1)S(1)} %get-tuple-element.9, bf16[64,32,64]{2,1,0:T(8,128)(2,1)S(1)} %get-tuple-element.8, bf16[64,32,64]{2,1,0:T(8,128)(2,1)S(1)} %get-tuple-element.6, pred[64,256]{1,0:T(8,128)(4,1)S(1)} %copy-done.19, ...), kind=kOutput, calls=%fused_computation.87 | convolution fusion | flops 71827456 | bytes 1622016 | tf_op jit(solution)/shard_map/nvj,kj->nvk/dot_general | solution.py:83
  141.6 2.0 %fusion.129 = f32[16,32,2,64]{3,1,2,0:T(8,128)} fusion(f32[16,32,64]{2,1,0:T(8,128)S(1)} %bitcast.376, bf16[16,32,64]{2,1,0:T(8,128)(2,1)S(1)} %get-tuple-element.44, bf16[16,32,64]{2,1,0:T(8,128)(2,1)S(1)} %get-tuple-element.43, bf16[16,32,64]{2,1,0:T(8,128)(2,1)S(1)} %get-tuple-element.42, bf16[16,32,64]{2,1,0:T(8,128)(2,1)S(1)} %get-tuple-element.41, ...), kind=kOutput, calls=%fused_computation.115 | convolution fusion | flops 26411008 | bytes 708608 | tf_op jit(solution)/shard_map/ksj,nvk->nsvj/dot_general | solution.py:91
  143.6 3.1 %fusion.127 = f32[32,32,2,64]{3,1,2,0:T(8,128)} fusion(f32[32,32,64]{2,1,0:T(8,128)} %bitcast.374, bf16[32,32,64]{2,1,0:T(8,128)(2,1)} %get-tuple-element.24, bf16[32,32,64]{2,1,0:T(8,128)(2,1)} %get-tuple-element.23, bf16[32,32,64]{2,1,0:T(8,128)(2,1)} %get-tuple-element.22, bf16[32,32,64]{2,1,0:T(8,128)(2,1)S(1)} %get-tuple-element.21, ...), kind=kOutput, calls=%fused_computation.113 | convolution fusion | flops 52822016 | bytes 2023424 | tf_op jit(solution)/shard_map/ksj,nvk->nsvj/dot_general | solution.py:91
  146.7 2.4 %fusion.358 = f32[32,32,64]{2,0,1:T(8,128)} fusion(bf16[32,64,64]{2,1,0:T(8,128)(2,1)} %bitcast.367, f32[64,32,64]{2,1,0:T(8,128)} %bitcast.372, s32[]{:T(128)S(6)} %select_n.77, f32[64,32,64]{2,1,0:T(8,128)} %fusion.103), kind=kOutput, calls=%fused_computation.318 | convolution fusion | flops 8392704 | bytes 819204 | tf_op jit(solution)/shard_map/dot_general | solution.py:134
  149.1 3.8 %fusion.84 = f32[32,32,256]{2,1,0:T(8,128)} fusion(f32[32,32,64]{2,0,1:T(8,128)} %fusion.358, bf16[2,32,64,512]{3,2,1,0:T(8,128)(2,1)} %param.21, bf16[32,32,512]{2,1,0:T(8,128)(2,1)S(1)} %copy-done.3, bf16[2,32,64,256]{3,2,1,0:T(8,128)(2,1)S(1)} %copy-done.2), kind=kOutput, calls=%fused_computation.55 | convolution fusion | flops 100794368 | bytes 5767168 | tf_op jit(solution)/shard_map/ikr,vik->vir/dot_general | solution.py:147
  152.9 1.5 pad_maximum_fusion.1
  154.5 2.1 %gather_fusion.2 = bf16[128,32,256]{2,1,0:T(8,128)(2,1)} fusion(bf16[32,96,256]{2,0,1:T(8,128)(2,1)S(1)} %pad_maximum_fusion.1, s32[1024]{0:T(1024)} %pad_clamp_fusion.1), kind=kCustom, calls=%fused_computation.2.clone | custom fusion | bytes 4194816 | tf_op jit(solution)/shard_map/jit(_take)/gather | solution.py:44
  156.6 1.9 %broadcast_select_fusion.1 = bf16[128,32,256]{2,1,0:T(8,128)(2,1)S(1)} fusion(bf16[128,32,256]{2,1,0:T(8,128)(2,1)} %gather_fusion.2, pred[128]{0:T(512)(128)(4,1)S(1)} %copy-done.28), kind=kLoop, calls=%fused_computation.21 | loop fusion | flops 1048576 | bytes 4194432 | tf_op jit(solution)/shard_map/jit(_take)/select_n | solution.py:44
  158.6 9.4 %fusion.58 = bf16[32,4,8,256]{3,2,1,0:T(8,128)(2,1)} fusion(f32[32,32,256]{2,1,0:T(8,128)S(1)} %copy-done.5, bf16[2,32,4,256,256]{4,3,2,1,0:T(8,128)(2,1)} %param.22, bf16[32,32,4,256]{3,0,2,1:T(8,128)(2,1)S(1)} %bitcast.365, pred[32,4]{1,0:T(8,128)(4,1)S(1)} %copy-done.25), kind=kOutput, calls=%fused_computation.38 | convolution fusion | flops 538443776 | bytes 20447360 | tf_op jit(solution)/shard_map/ijrc,vijc->vir/dot_general | solution.py:54
  168.0 1.9 %copy.116 = bf16[32,4,8,256]{3,2,0,1:T(8,128)(2,1)} copy(bf16[32,4,8,256]{3,2,1,0:T(8,128)(2,1)} %fusion.58) | data formatting | bytes 1048576 | tf_op jit(solution)/shard_map/reshape | solution.py:153
  (188 shorter events, 40.9 us)
Async XLA Ops:
  0.0 8.9 %copy-start.7 = (bf16[32,8192]{1,0:T(8,128)(2,1)S(1)}, bf16[32,8192]{1,0:T(8,128)(2,1)}, u32[]{:S(2)}) copy-start(bf16[32,8192]{1,0:T(8,128)(2,1)} %param.16) | copy-start | bytes 1572868
  0.0 15.9 %copy-start.8 = (bf16[2,64,2048]{2,1,0:T(8,128)(2,1)S(1)}, bf16[2,64,2048]{2,1,0:T(8,128)(2,1)}, u32[]{:S(2)}) copy-start(bf16[2,64,2048]{2,1,0:T(8,128)(2,1)} %param.18) | copy-start | bytes 1572868
  1.9 46.0 %collective-permute-start.3 = (bf16[32,32,64]{2,0,1:T(8,128)(2,1)S(1)}, bf16[32,32,64]{2,0,1:T(8,128)(2,1)S(1)}, u32[]{:S(2)}, u32[]{:S(2)}) collective-permute-start(bf16[32,32,64]{2,0,1:T(8,128)(2,1)S(1)} %fusion.78), channel_id=1, source_target_pairs={{4,0},{8,4},{12,8},{16,12},{20,16},{24,20},{28,24},{32,28},{36,32}... | collective-permute-start | bytes 393224 | tf_op jit(solution)/shard_map/ppermute | solution.py:36
  7.0 40.9 %collective-permute-start.2 = (bf16[32,32,64]{2,0,1:T(8,128)(2,1)S(1)}, bf16[32,32,64]{2,0,1:T(8,128)(2,1)S(1)}, u32[]{:S(2)}, u32[]{:S(2)}) collective-permute-start(bf16[32,32,64]{2,0,1:T(8,128)(2,1)S(1)} %fusion.78), channel_id=1, source_target_pairs={{0,4},{4,8},{8,12},{12,16},{16,20},{20,24},{24,28},{28,32},{32,36}... | collective-permute-start | bytes 393224 | tf_op jit(solution)/shard_map/ppermute | solution.py:34
  9.8 22.4 %copy-start.20 = (s32[5,64,4]{1,2,0:T(4,128)S(1)}, s32[5,64,4]{1,2,0:T(4,128)}, u32[]{:S(2)}) copy-start(s32[5,64,4]{1,2,0:T(4,128)} %param.23) | copy-start | bytes 15364
  9.8 22.5 %copy-start.26 = (s32[32,8]{0,1:T(8,128)S(1)}, s32[32,8]{0,1:T(8,128)}, u32[]{:S(2)}) copy-start(s32[32,8]{0,1:T(8,128)} %param.24) | copy-start | bytes 3076
  9.8 23.3 %copy-start.33 = (s32[32,4]{0,1:T(4,128)S(1)}, s32[32,4]{0,1:T(4,128)}, u32[]{:S(2)}) copy-start(s32[32,4]{0,1:T(4,128)} %param.26) | copy-start | bytes 1540
  9.8 24.0 %copy-start.10 = (bf16[2,4,64,128]{3,2,1,0:T(8,128)(2,1)S(1)}, bf16[2,4,64,128]{3,2,1,0:T(8,128)(2,1)}, u32[]{:S(2)}) copy-start(bf16[2,4,64,128]{3,2,1,0:T(8,128)(2,1)} %param.19) | copy-start | bytes 393220
  9.8 62.9 %collective-permute-start.1 = (bf16[32,32,256]{2,0,1:T(8,128)(2,1)}, bf16[32,32,256]{2,0,1:T(8,128)(2,1)}, u32[]{:S(2)}, u32[]{:S(2)}) collective-permute-start(bf16[32,32,256]{2,0,1:T(8,128)(2,1)} %bitcast.360), channel_id=1, source_target_pairs={{4,0},{8,4},{12,8},{16,12},{20,16},{24,20},{28,24},{32,28},{36,32}... | collective-permute-start | bytes 1572872 | tf_op jit(solution)/shard_map/ppermute | solution.py:36
  12.4 60.4 %collective-permute-start = (bf16[32,32,256]{2,0,1:T(8,128)(2,1)}, bf16[32,32,256]{2,0,1:T(8,128)(2,1)}, u32[]{:S(2)}, u32[]{:S(2)}) collective-permute-start(bf16[32,32,256]{2,0,1:T(8,128)(2,1)} %bitcast.360), channel_id=1, source_target_pairs={{0,4},{4,8},{8,12},{12,16},{16,20},{20,24},{24,28},{28,32},{32,36}... | collective-permute-start | bytes 1572872 | tf_op jit(solution)/shard_map/ppermute | solution.py:34
  15.6 18.2 %copy-start.36 = (s32[32]{0:T(128)S(1)}, s32[32]{0:T(128)}, u32[]{:S(2)}) copy-start(s32[32]{0:T(128)} %param.25) | copy-start | bytes 388
  15.7 18.2 %copy-start.37 = (s32[32]{0:T(128)S(1)}, s32[32]{0:T(128)}, u32[]{:S(2)}) copy-start(s32[32]{0:T(128)} %param.27) | copy-start | bytes 388
  17.2 36.3 %all-to-all-start = ((bf16[64,2,1024]{2,1,0:T(2,128)(2,1)}), bf16[64,2,1024]{2,1,0:T(2,128)(2,1)S(1)}, u32[]{:S(2)}, u32[]{:S(2)}) async-start(bf16[64,2,1024]{2,1,0:T(2,128)(2,1)} %reshape.283), calls=%async_computation | async-start | bytes 524288 | tf_op jit(solution)/shard_map/all_to_all | solution.py:17
  56.5 4.9 %copy-start.17 = (bf16[64,2,64]{2,1,0:T(2,128)(2,1)S(1)}, bf16[64,2,64]{2,1,0:T(2,128)(2,1)}, u32[]{:S(2)}) copy-start(bf16[64,2,64]{2,1,0:T(2,128)(2,1)} %reshape_squeeze.26) | copy-start | bytes 49156
  56.5 4.9 %copy-start.22 = (pred[16,256]{1,0:T(8,128)(4,1)S(1)}, pred[16,256]{1,0:T(8,128)(4,1)}, u32[]{:S(2)}) copy-start(pred[16,256]{1,0:T(8,128)(4,1)} %gt.83) | copy-start | bytes 12292
  63.4 5.5 %copy-start = (bf16[2,32,64,256]{3,2,1,0:T(8,128)(2,1)S(1)}, bf16[2,32,64,256]{3,2,1,0:T(8,128)(2,1)}, u32[]{:S(2)}) copy-start(bf16[2,32,64,256]{3,2,1,0:T(8,128)(2,1)} %param.17) | copy-start | bytes 6291460
  63.4 5.5 %copy-start.4 = (bf16[32,32,512]{2,1,0:T(8,128)(2,1)S(1)}, bf16[32,32,512]{2,1,0:T(8,128)(2,1)}, u32[]{:S(2)}) copy-start(bf16[32,32,512]{2,1,0:T(8,128)(2,1)} %broadcast_select_fusion.3) | copy-start | bytes 3145732
  79.7 12.3 %copy-start.1 = (bf16[2,32,64,256]{3,2,1,0:T(8,128)(2,1)S(1)}, bf16[2,32,64,256]{3,2,1,0:T(8,128)(2,1)}, u32[]{:S(2)}) copy-start(bf16[2,32,64,256]{3,2,1,0:T(8,128)(2,1)} %param.17) | copy-start | bytes 6291460
  92.1 13.0 %copy-start.9 = (bf16[2,64,2048]{2,1,0:T(8,128)(2,1)S(1)}, bf16[2,64,2048]{2,1,0:T(8,128)(2,1)}, u32[]{:S(2)}) copy-start(bf16[2,64,2048]{2,1,0:T(8,128)(2,1)} %param.18) | copy-start | bytes 1572868
  93.7 27.0 %collective-permute-start.7 = (bf16[32,32,64]{2,0,1:T(8,128)(2,1)S(1)}, bf16[32,32,64]{2,0,1:T(8,128)(2,1)S(1)}, u32[]{:S(2)}, u32[]{:S(2)}) collective-permute-start(bf16[32,32,64]{2,0,1:T(8,128)(2,1)S(1)} %fusion.79), channel_id=1, source_target_pairs={{4,0},{8,4},{12,8},{16,12},{20,16},{24,20},{28,24},{32,28},{36,32}... | collective-permute-start | bytes 393224 | tf_op jit(solution)/shard_map/ppermute | solution.py:36
  96.1 24.6 %collective-permute-start.6 = (bf16[32,32,64]{2,0,1:T(8,128)(2,1)S(1)}, bf16[32,32,64]{2,0,1:T(8,128)(2,1)S(1)}, u32[]{:S(2)}, u32[]{:S(2)}) collective-permute-start(bf16[32,32,64]{2,0,1:T(8,128)(2,1)S(1)} %fusion.79), channel_id=1, source_target_pairs={{0,4},{4,8},{8,12},{12,16},{16,20},{20,24},{24,28},{28,32},{32,36}... | collective-permute-start | bytes 393224 | tf_op jit(solution)/shard_map/ppermute | solution.py:34
  99.3 53.7 %collective-permute-start.5 = (bf16[32,32,256]{2,0,1:T(8,128)(2,1)}, bf16[32,32,256]{2,0,1:T(8,128)(2,1)}, u32[]{:S(2)}, u32[]{:S(2)}) collective-permute-start(bf16[32,32,256]{2,0,1:T(8,128)(2,1)} %fusion.63), channel_id=1, source_target_pairs={{4,0},{8,4},{12,8},{16,12},{20,16},{24,20},{28,24},{32,28},{36,32}... | collective-permute-start | bytes 1572872 | tf_op jit(solution)/shard_map/ppermute | solution.py:36
  101.2 51.7 %collective-permute-start.4 = (bf16[32,32,256]{2,0,1:T(8,128)(2,1)}, bf16[32,32,256]{2,0,1:T(8,128)(2,1)}, u32[]{:S(2)}, u32[]{:S(2)}) collective-permute-start(bf16[32,32,256]{2,0,1:T(8,128)(2,1)} %fusion.63), channel_id=1, source_target_pairs={{0,4},{4,8},{8,12},{12,16},{16,20},{20,24},{24,28},{28,32},{32,36}... | collective-permute-start | bytes 1572872 | tf_op jit(solution)/shard_map/ppermute | solution.py:34
  106.4 27.3 %all-to-all-start.1 = ((bf16[64,2,1024]{2,1,0:T(2,128)(2,1)}), bf16[64,2,1024]{2,1,0:T(2,128)(2,1)S(1)}, u32[]{:S(2)}, u32[]{:S(2)}) async-start(bf16[64,2,1024]{2,1,0:T(2,128)(2,1)} %reshape.285), calls=%async_computation.1 | async-start | bytes 524288 | tf_op jit(solution)/shard_map/all_to_all | solution.py:17
  136.6 3.8 %copy-start.13 = (bf16[64,2,64]{2,1,0:T(2,128)(2,1)S(1)}, bf16[64,2,64]{2,1,0:T(2,128)(2,1)}, u32[]{:S(2)}) copy-start(bf16[64,2,64]{2,1,0:T(2,128)(2,1)} %reshape_squeeze.29) | copy-start | bytes 49156
  136.6 3.8 %copy-start.32 = (pred[8,256]{1,0:T(8,128)(4,1)S(1)}, pred[8,256]{1,0:T(8,128)(4,1)}, u32[]{:S(2)}) copy-start(pred[8,256]{1,0:T(8,128)(4,1)} %gt.86) | copy-start | bytes 6148
  136.6 4.9 %copy-start.12 = (bf16[64,2,64]{2,1,0:T(2,128)(2,1)S(1)}, bf16[64,2,64]{2,1,0:T(2,128)(2,1)}, u32[]{:S(2)}) copy-start(bf16[64,2,64]{2,1,0:T(2,128)(2,1)} %reshape_squeeze.30) | copy-start | bytes 49156
  136.6 4.9 %copy-start.23 = (pred[16,256]{1,0:T(8,128)(4,1)S(1)}, pred[16,256]{1,0:T(8,128)(4,1)}, u32[]{:S(2)}) copy-start(pred[16,256]{1,0:T(8,128)(4,1)} %gt.83) | copy-start | bytes 12292
  139.3 4.3 %copy-start.11 = (bf16[64,2,64]{2,1,0:T(2,128)(2,1)S(1)}, bf16[64,2,64]{2,1,0:T(2,128)(2,1)}, u32[]{:S(2)}) copy-start(bf16[64,2,64]{2,1,0:T(2,128)(2,1)} %reshape_squeeze.31) | copy-start | bytes 49156
  139.3 4.3 %copy-start.21 = (pred[32,256]{1,0:T(8,128)(4,1)S(1)}, pred[32,256]{1,0:T(8,128)(4,1)}, u32[]{:S(2)}) copy-start(pred[32,256]{1,0:T(8,128)(4,1)} %gt.80) | copy-start | bytes 24580
  143.6 5.5 %copy-start.2 = (bf16[2,32,64,256]{3,2,1,0:T(8,128)(2,1)S(1)}, bf16[2,32,64,256]{3,2,1,0:T(8,128)(2,1)}, u32[]{:S(2)}) copy-start(bf16[2,32,64,256]{3,2,1,0:T(8,128)(2,1)} %param.17) | copy-start | bytes 6291460
  143.6 5.5 %copy-start.3 = (bf16[32,32,512]{2,1,0:T(8,128)(2,1)S(1)}, bf16[32,32,512]{2,1,0:T(8,128)(2,1)}, u32[]{:S(2)}) copy-start(bf16[32,32,512]{2,1,0:T(8,128)(2,1)} %broadcast_select_fusion.2) | copy-start | bytes 3145732
  (16 other events, 38.5 us)
where the time goes:
time: 171 us; the launch traced here: 170 us
  matrix products  59.7 us (35%)
  starting transfers between devices  53 us (31%)
  local copies, waits for them, and re-layouts  32.9 us (19%)
  other arithmetic  15.7 us (9%)
  waiting for transfers between devices  7.62 us (4%)
    all_to_all x2, starting transfers between devices, from_everyone(): lax.all_to_all(jnp.broadcast_to(value[None], (length, *value.shape)), axi...  29.1 us
    dot_general x2, matrix products, near_product(): jnp.einsum('ijrc,vijc->vir', dense_blocks, picked, preferred_element_type...  21.7 us
    dot_general x8, matrix products, tree_gathered(): jnp.einsum('ksj,nvk->nsvj', joined, descent.astype(jnp.bfloat16), preferr...  14.6 us
    ppermute x4, starting transfers between devices, padded_2(): lax.ppermute(head, axis, [((i + 1) % count, i) for i in range(ends)])  11.9 us
    ppermute x4, starting transfers between devices, padded_2(): lax.ppermute(tail, axis, [(i, (i + 1) % count) for i in range(ends)])  11.9 us
    dot_general x2, matrix products, apply_matrix(): jnp.einsum('ikr,vik->vir', basis[matrix_index], leaf_round, preferred_ele...  7.63 us
    all_to_all x2, waiting for transfers between devices, from_everyone(): lax.all_to_all(jnp.broadcast_to(value[None], (length, *value.shape)), axi...  7.6 us
    select_n x6, other arithmetic, pick_rows(): picked = jnp.take(source, leaf_index.reshape(-1), axis=1)  7.09 us
  transfers between devices with their start and end apart: 10, of which 1 were waited for; matrix products, arithmetic and copies ran while one was open for 40% of the time, Pallas kernels for 0%

commit v1 on v0

v1 whole, which is shorter than its diff:
```python
import jax
import jax.numpy as jnp
from jax import lax
from jax.experimental import pallas as pl
from jax.experimental.pallas import tpu as pltpu
from jax.sharding import PartitionSpec as P

OFFSETS = (-3, -2, 2, 3)
PLANE = 8
PLANES = 8
LEAF_DEV = 32
LEAF = 256
RANK = 64
COLS = 32
CHUNKS = 8
NT = (((1,), (1,)), ((), ()))
NN = (((1,), (0,)), ((), ()))


def dot_nt(a, b):
    return lax.dot_general(a, b, NT, preferred_element_type=jnp.float32)


def dot_nn(a, b):
    return lax.dot_general(a, b, NN, preferred_element_type=jnp.float32)


def kernel(
    far_mask, far_ids, far_count, near_ids, near_count,
    vectors, basis, leaf_transfer, upper_transfer, upper_coupling, leaf_coupling, near_blocks,
    out,
    near_w, coup_w, basis_w, trans_w, up_t, up_c,
    va, vb, cpa, cpb, dl, dr, near_acc, field,
    l0, l1, l2, l3, l4, cc,
    sem_near, sem_in,
    v_send, v_recv, c_send, c_recv, p_send, p_recv, z_send, z_recv, e_send, e_recv,
):
    b = lax.axis_index("branch")
    col = lax.axis_index("col")
    z = b // PLANE
    j = lax.rem(b, PLANE)
    core = lax.rem(b, 2)
    x = j // 2
    first_leaf = (b - 1) * LEAF_DEV
    lane = lax.broadcasted_iota(jnp.int32, (COLS, 128), 1)
    left = lane < 64

    def local(src, dst, sem):
        copy = pltpu.make_async_copy(src, dst, sem)
        copy.start()
        return copy

    def load_leaf(i, carry):
        local(vectors.at[:, pl.ds(pl.multiple_of(i * LEAF, LEAF), LEAF)], va.at[LEAF_DEV + i], sem_in.at[0])
        return carry

    lax.fori_loop(0, LEAF_DEV, load_leaf, 0, unroll=4)
    own = pl.ds(LEAF_DEV, LEAF_DEV)
    load_v = pltpu.make_async_copy(va.at[own], va.at[own], sem_in.at[0])
    load_basis = [None, None]
    load_trans = [None, None]
    load_coup = [None, None]
    load_near = [[], []]
    load_basis[0] = local(basis.at[0], basis_w.at[0], sem_in.at[1])
    load_trans[0] = local(leaf_transfer.at[0], trans_w.at[0], sem_in.at[2])
    load_ut = local(upper_transfer, up_t, sem_in.at[3])
    load_uc = local(upper_coupling, up_c, sem_in.at[4])
    step = LEAF_DEV // CHUNKS
    for m in range(2):
        if m == 1:
            load_basis[1] = local(basis.at[1], basis_w.at[1], sem_in.at[5])
            load_trans[1] = local(leaf_transfer.at[1], trans_w.at[1], sem_in.at[6])
        for g in range(CHUNKS):
            part = pl.ds(g * step, step)
            load_near[m].append(local(near_blocks.at[m, part], near_w.at[m, part], sem_near.at[m, g]))
            if g == 1:
                load_coup[m] = local(leaf_coupling.at[m], coup_w.at[m], sem_in.at[7 + m])

    barrier = pltpu.get_barrier_semaphore()

    def greet(target):
        pl.semaphore_signal(barrier, inc=1, device_id=(target, col), device_id_type=pl.DeviceIdType.MESH)

    plane_peer = [z * PLANE + lax.rem(j + d, PLANE) for d in range(PLANE)]
    z_peer = [lax.rem(z + d, PLANES) * PLANE + j for d in range(PLANES)]

    @pl.when(b > 0)
    def _():
        greet(b - 1)

    @pl.when(b < PLANE * PLANES - 1)
    def _():
        greet(b + 1)

    for d in range(1, PLANE):
        greet(plane_peer[d])
    for d in range(1, PLANES):
        greet(z_peer[d])

    va[96] = jnp.zeros((COLS, LEAF), jnp.bfloat16)
    vb[96] = jnp.zeros((COLS, LEAF), jnp.bfloat16)
    dl[96] = jnp.zeros((COLS, 128), jnp.bfloat16)
    dr[96] = jnp.zeros((COLS, 128), jnp.bfloat16)

    def remote(src, dst, send, recv, target):
        return pltpu.make_async_remote_copy(
            src_ref=src, dst_ref=dst, send_sem=send, recv_sem=recv,
            device_id=(target, col), device_id_type=pl.DeviceIdType.MESH,
        )

    def halo_sends(m, mine, to_right, to_left, send, recv):
        return (
            remote(mine, to_right, send.at[m, 0], recv.at[m, 0], b + 1),
            remote(mine, to_left, send.at[m, 1], recv.at[m, 1], b - 1),
        )

    has_right = b < PLANE * PLANES - 1
    has_left = b > 0

    def halo_start(copies):
        @pl.when(has_right)
        def _():
            copies[0].start()

        @pl.when(has_left)
        def _():
            copies[1].start()

    def halo_recv(copies):
        @pl.when(has_left)
        def _():
            copies[0].wait_recv()

        @pl.when(has_right)
        def _():
            copies[1].wait_recv()

    def halo_sent(copies):
        @pl.when(has_right)
        def _():
            copies[0].wait_send()

        @pl.when(has_left)
        def _():
            copies[1].wait_send()

    def halves(pair):
        turned = pltpu.roll(pair, 64, 1)
        none = jnp.zeros_like(pair)
        return (
            jnp.where(left, pair, none).astype(jnp.bfloat16),
            jnp.where(left, none, turned).astype(jnp.bfloat16),
            jnp.where(left, turned, none).astype(jnp.bfloat16),
            jnp.where(left, none, pair).astype(jnp.bfloat16),
        )

    def put_halves(leaf, pair):
        al, ar, bl, br = halves(pair)
        dl[leaf] = al
        dr[leaf] = ar
        dl[leaf + 1] = bl
        dr[leaf + 1] = br

    def coef_pair(m, source, cp, p):
        lhs = source[pl.ds(LEAF_DEV + 2 * p, 2)].reshape(2 * COLS, LEAF)
        rhs = basis_w[m, pl.ds(2 * p, 2)].reshape(128, LEAF)
        both = dot_nt(lhs, rhs)
        got = jnp.where(left, both[:COLS], both[COLS:])
        cp[:, pl.ds(pl.multiple_of(LEAF_DEV * RANK + p * 128, 128), 128)] = got.astype(jnp.bfloat16)
        put_halves(LEAF_DEV + 2 * p, got)

    def masked_half(both, parity):
        keep = jnp.logical_xor(left, parity == 1)
        return jnp.where(keep, both, jnp.zeros_like(both)).astype(jnp.bfloat16)

    def live_or_zero(q, count, leaf):
        dead = lax.shift_right_arithmetic(q - count, 31) + 1
        return (leaf - first_leaf) + dead * (96 - (leaf - first_leaf))

    for m in range(2):
        source = va if m == 0 else vb
        cp = cpa if m == 0 else cpb
        if m == 0:
            load_v.wait()
            load_basis[0].wait()

            def coef_body(p, carry):
                coef_pair(0, va, cpa, p)
                return carry

            lax.fori_loop(0, LEAF_DEV // 2, coef_body, 0, unroll=2)
        load_trans[m].wait()
        box = dot_nt(cp[:, pl.ds(LEAF_DEV * RANK, LEAF_DEV * RANK)], trans_w[m])
        l0[m, 3 + j] = masked_half(jnp.concatenate([box, box], axis=1), core)
        if m == 0:
            last = PLANE * PLANES - 1
            pl.semaphore_wait(barrier, 14 + (b + last) // (last + 1) + (2 * last - b) // (last + 1))
        plane = []
        for d in range(1, PLANE):
            copy = remote(l0.at[m, 3 + j], l0.at[m, 3 + j], p_send.at[m, d], p_recv.at[m, d], plane_peer[d])
            copy.start()
            plane.append(copy)
        flat = LEAF_DEV * RANK
        coef_halo = halo_sends(
            m, cp.at[:, pl.ds(flat, flat)], cp.at[:, pl.ds(0, flat)], cp.at[:, pl.ds(2 * flat, flat)], c_send, c_recv
        )
        halo_start(coef_halo)
        vec_halo = halo_sends(
            m, source.at[own], source.at[pl.ds(0, LEAF_DEV)], source.at[pl.ds(2 * LEAF_DEV, LEAF_DEV)], v_send, v_recv
        )
        halo_start(vec_halo)

        if m == 0:
            load_ut.wait()
            load_uc.wait()
            for mm in range(2):
                for h in range(5):
                    blocks = []
                    for q in range(4):
                        one = up_c[mm, h, :, q * RANK:(q + 1) * RANK]
                        blocks += [one, one]
                    cc[mm, h] = jnp.concatenate(blocks, axis=1)

        for g in range(CHUNKS):
            load_near[m][g].wait()

        def own_body(i, carry):
            piece = source[LEAF_DEV + i]
            near_acc[:, pl.ds(pl.multiple_of(i * LEAF, LEAF), LEAF)] = dot_nt(piece, near_w[m, i, 0])
            return carry

        lax.fori_loop(0, LEAF_DEV, own_body, 0, unroll=2)

        for copy in plane:
            copy.wait_recv()

        def lift(pairs, h):
            weight = up_t[m, h]
            return dot_nt(pairs, jnp.concatenate([weight, weight], axis=0))

        pairs = jnp.concatenate([l0[m, 3 + 2 * i] + l0[m, 4 + 2 * i] for i in range(4)], axis=0)
        lifted = lift(pairs, 0)
        n1 = [masked_half(lifted[i * COLS:(i + 1) * COLS], i % 2) for i in range(4)]
        for i in range(4):
            l1[m, 3 + i] = n1[i]
        lifted = lift(jnp.concatenate([n1[0] + n1[1], n1[2] + n1[3]], axis=0), 1)
        n2 = [masked_half(lifted[i * COLS:(i + 1) * COLS], i % 2) for i in range(2)]
        for i in range(2):
            l2[m, 4 + i] = n2[i]
        l3[m, z] = masked_half(lift(n2[0] + n2[1], 2), lax.rem(z, 2))

        across = []
        for d in range(1, PLANES):
            copy = remote(l3.at[m, z], l3.at[m, z], z_send.at[m, d], z_recv.at[m, d], z_peer[d])
            copy.start()
            across.append(copy)
        up_one = b + PLANE
        down_one = b - PLANE
        up_two = b + 2 * PLANE
        down_two = b - 2 * PLANE

        def edge(k, src, dst, target):
            return remote(src, dst, e_send.at[m, k], e_recv.at[m, k], target)

        ups = [
            edge(0, l2.at[m, pl.ds(4, 2)], l2.at[m, pl.ds(2, 2)], up_one),
            edge(1, l1.at[m, pl.ds(4, 3)], l1.at[m, pl.ds(0, 3)], up_one),
            edge(2, l0.at[m, pl.ds(8, 3)], l0.at[m, pl.ds(0, 3)], up_one),
        ]
        downs = [
            edge(3, l2.at[m, pl.ds(4, 2)], l2.at[m, pl.ds(6, 2)], down_one),
            edge(4, l1.at[m, pl.ds(3, 3)], l1.at[m, pl.ds(7, 3)], down_one),
            edge(5, l0.at[m, pl.ds(3, 3)], l0.at[m, pl.ds(11, 3)], down_one),
        ]
        up2 = edge(6, l2.at[m, pl.ds(4, 2)], l2.at[m, pl.ds(0, 2)], up_two)
        down2 = edge(7, l2.at[m, pl.ds(4, 2)], l2.at[m, pl.ds(8, 2)], down_two)

        @pl.when(z + 1 < PLANES)
        def _():
            for copy in ups:
                copy.start()

        @pl.when(z > 0)
        def _():
            for copy in downs:
                copy.start()

        @pl.when(z + 2 < PLANES)
        def _():
            up2.start()

        @pl.when(z > 1)
        def _():
            down2.start()

        halo_recv(coef_halo)

        def dup_body(p, carry):
            for spot in (p, p + LEAF_DEV):
                pair = cp[:, pl.ds(pl.multiple_of(spot * 128, 128), 128)].astype(jnp.float32)
                put_halves(2 * spot, pair)
            return carry

        lax.fori_loop(0, LEAF_DEV // 2, dup_body, 0)
        load_coup[m].wait()

        def far_rows(i):
            count = far_count[i]

            def spot(q):
                return live_or_zero(q, count, far_ids[q, i])

            return jnp.concatenate([dl[spot(2 * t)] + dr[spot(2 * t + 1)] for t in range(4)], axis=1)

        def coup_body(p, carry):
            lhs = jnp.concatenate([far_rows(2 * p), far_rows(2 * p + 1)], axis=0)
            rhs = coup_w[m, pl.ds(2 * p, 2)].reshape(128, 512)
            both = dot_nt(lhs, rhs)
            field[:, pl.ds(pl.multiple_of(p * 128, 128), 128)] = jnp.where(left, both[:COLS], both[COLS:])
            return carry

        lax.fori_loop(0, LEAF_DEV // 2, coup_body, 0, unroll=1)

        halo_recv(vec_halo)

        def near_body(i, carry):
            where_to = pl.ds(pl.multiple_of(i * LEAF, LEAF), LEAF)
            total = near_acc[:, where_to]
            count = near_count[i]
            for q in range(1, 4):
                spot = live_or_zero(q, count, near_ids[q, i])
                piece = source[spot]
                total = total + dot_nt(piece, near_w[m, i, q])
            near_acc[:, where_to] = total
            return carry

        lax.fori_loop(0, LEAF_DEV, near_body, 0, unroll=2)

        for copy in across:
            copy.wait_recv()

        @pl.when(z + 1 < PLANES)
        def _():
            for copy in downs:
                copy.wait_recv()

        @pl.when(z > 0)
        def _():
            for copy in ups:
                copy.wait_recv()

        @pl.when(z + 2 < PLANES)
        def _():
            down2.wait_recv()

        @pl.when(z > 1)
        def _():
            up2.wait_recv()

        pairs = jnp.concatenate([l3[m, 2 * i] + l3[m, 2 * i + 1] for i in range(4)], axis=0)
        lifted = lift(pairs, 3)
        for i in range(4):
            l4[i] = masked_half(lifted[i * COLS:(i + 1) * COLS], 0)

        def node(h, o):
            if h == 0:
                return l0[m, 3 + j + o]
            if h == 1:
                return l1[m, 3 + x + o]
            if h == 2:
                return l2[m, 4 + x // 2 + o]
            if h == 3:
                return l3[m, lax.rem(z + o + PLANES, PLANES)]
            return l4[lax.rem(z // 2 + o + 4, 4)]

        def coupled(h):
            n = b // (1 << h)
            blocks = []
            for q, o in enumerate(OFFSETS):
                there = jnp.logical_and(n + o >= 0, n + o < (64 >> h))
                live = jnp.full((COLS, 128), far_mask[h, q, n].astype(jnp.float32)).astype(jnp.bfloat16)
                blocks.append(jnp.where(there, node(h, o), jnp.zeros((COLS, 128), jnp.bfloat16)) * live)
            return dot_nt(jnp.concatenate(blocks, axis=1), cc[m, h])

        descent = coupled(4)
        for h in (3, 2, 1, 0):
            both = dot_nn(descent.astype(jnp.bfloat16), up_t[m, h])
            side = lax.rem(b // (1 << h), 2)
            descent = coupled(h) + jnp.where(side == 0, both[:, :RANK], both[:, RANK:])
        parent = descent.astype(jnp.bfloat16)
        field[...] += dot_nn(parent, trans_w[m])

        def final_body(p, carry):
            pair = field[:, pl.ds(pl.multiple_of(p * 128, 128), 128)]
            none = jnp.zeros_like(pair)
            lhs = jnp.concatenate([jnp.where(left, pair, none), jnp.where(left, none, pair)], axis=0).astype(jnp.bfloat16)
            rhs = basis_w[m, pl.ds(2 * p, 2)].reshape(128, LEAF)
            both = dot_nn(lhs, rhs)
            total = near_acc[:, pl.ds(pl.multiple_of(p * 512, 512), 512)]
            first = (total[:, :LEAF] + both[:COLS]).astype(jnp.bfloat16)
            second = (total[:, LEAF:] + both[COLS:]).astype(jnp.bfloat16)
            if m == 0:
                vb[LEAF_DEV + 2 * p] = first
                vb[LEAF_DEV + 2 * p + 1] = second
                coef_pair(1, vb, cpb, p)
            else:
                out[:, pl.ds(pl.multiple_of(p * 512, 512), LEAF)] = first
                out[:, pl.ds(pl.multiple_of(p * 512 + LEAF, LEAF), LEAF)] = second
            return carry

        if m == 0:
            load_basis[1].wait()
        lax.fori_loop(0, LEAF_DEV // 2, final_body, 0, unroll=2)

        for copy in plane + across:
            copy.wait_send()
        halo_sent(coef_halo)
        halo_sent(vec_halo)

        @pl.when(z + 1 < PLANES)
        def _():
            for copy in ups:
                copy.wait_send()

        @pl.when(z > 0)
        def _():
            for copy in downs:
                copy.wait_send()

        @pl.when(z + 2 < PLANES)
        def _():
            up2.wait_send()

        @pl.when(z > 1)
        def _():
            down2.wait_send()


def shards(
    vectors, basis, leaf_transfer, upper_transfer, upper_coupling, leaf_coupling, near_blocks,
    far_mask, far_ids, far_count, near_ids, near_count,
):
    smem = pl.BlockSpec(memory_space=pltpu.SMEM)
    hbm = pl.BlockSpec(memory_space=pl.ANY)
    bf = jnp.bfloat16
    f32 = jnp.float32
    dma = pltpu.SemaphoreType.DMA
    return pl.pallas_call(
        kernel,
        out_shape=jax.ShapeDtypeStruct((COLS, LEAF_DEV * LEAF), bf),
        in_specs=[smem] * 5 + [hbm] * 7,
        out_specs=pl.BlockSpec(memory_space=pltpu.VMEM),
        scratch_shapes=[
            pltpu.VMEM((2, LEAF_DEV, 4, LEAF, LEAF), bf),
            pltpu.VMEM((2, LEAF_DEV, RANK, 512), bf),
            pltpu.VMEM((2, LEAF_DEV, RANK, LEAF), bf),
            pltpu.VMEM((2, RANK, LEAF_DEV * RANK), bf),
            pltpu.VMEM((2, 4, RANK, 128), bf),
            pltpu.VMEM((2, 5, RANK, 256), bf),
            pltpu.VMEM((97, COLS, LEAF), bf),
            pltpu.VMEM((97, COLS, LEAF), bf),
            pltpu.VMEM((COLS, 96 * RANK), bf),
            pltpu.VMEM((COLS, 96 * RANK), bf),
            pltpu.VMEM((97, COLS, 128), bf),
            pltpu.VMEM((97, COLS, 128), bf),
            pltpu.VMEM((COLS, LEAF_DEV * LEAF), f32),
            pltpu.VMEM((COLS, LEAF_DEV * RANK), f32),
            pltpu.VMEM((2, 14, COLS, 128), bf),
            pltpu.VMEM((2, 10, COLS, 128), bf),
            pltpu.VMEM((2, 10, COLS, 128), bf),
            pltpu.VMEM((2, 8, COLS, 128), bf),
            pltpu.VMEM((4, COLS, 128), bf),
            pltpu.VMEM((2, 5, RANK, 512), bf),
            dma((2, CHUNKS)), dma((9,)),
            dma((2, 2)), dma((2, 2)), dma((2, 2)), dma((2, 2)),
            dma((2, 8)), dma((2, 8)), dma((2, 8)), dma((2, 8)), dma((2, 8)), dma((2, 8)),
        ],
        compiler_params=pltpu.CompilerParams(
            collective_id=0, has_side_effects=True, vmem_limit_bytes=60 << 20
        ),
        name="product",
    )(
        jnp.transpose(far_mask, (0, 2, 1)), far_ids.T, far_count, near_ids.T, near_count,
        vectors, basis, leaf_transfer, upper_transfer, upper_coupling, leaf_coupling, near_blocks,
    )


def solution(mesh):
    return jax.shard_map(
        shards,
        mesh=mesh,
        in_specs=(
            P("col", "branch"),
            P(None, "branch", None, None),
            P(None, None, "branch"),
            P(),
            P(),
            P(None, "branch", None, None),
            P(None, "branch", None, None, None),
            P(),
            P("branch", None),
            P("branch"),
            P("branch", None),
            P("branch"),
        ),
        out_specs=P("col", "branch"),
        check_vma=False,
    )
```

time: 171 us -> 59.7 us (0.35)
  the two profiles are of different devices: /device:TPU:1 before, /device:TPU:39 now
where the time goes in v1:
time: 59.7 us; the launch traced here: 59.6 us
  Pallas kernels  57.7 us (97%)
  local copies, waits for them, and re-layouts  1.87 us (3%)
    pallas_call x1, Pallas kernels, shards(): pl.pallas_call(kernel, out_shape=jax.ShapeDtypeStruct((COLS, LEAF_DEV * L...  57.7 us
    unnamed x1, local copies, waits for them, and re-layouts  1.87 us

profile of v1, /device:TPU:39, one launch (start us, length us, event | category | flops | bytes accessed | tf_op | source)
XLA Modules:
  0.0 59.6 jit_solution(16940090672482069016)
XLA Ops:
  0.0 57.7 %product.1 = bf16[32,8192]{1,0:T(8,128)(2,1)} custom-call(s32[5,4,64]{2,1,0:T(4,128)} %bitcast.3, s32[8,32]{1,0:T(8,128)} %bitcast.4, s32[32]{0:T(128)} %far_count.1, s32[4,32]{1,0:T(4,128)} %bitcast.5, s32[32]{0:T(128)} %near_count.1, bf16[32,8192]{1,0:T(8,128)(2,1)} %vectors.1, bf16[2,32,64,256]{3,2,1,0:T(8,128)(2,1)} %basis.1, ...), custom_call_target="tpu_custom_call" | custom-call | tf_op jit(solution)/shard_map/product/pallas_call | solution.py:448
  57.7 1.9 %copy.14 = bf16[32,8192]{1,0:T(8,128)(2,1)} copy(bf16[32,8192]{1,0:T(8,128)(2,1)} %product.1) | data formatting | bytes 1048576

commit v2 on v1

--- a/solution.py
+++ b/solution.py
@@ -13,6 +13,8 @@
 RANK = 64
 COLS = 32
 CHUNKS = 8
+STEP = LEAF_DEV // CHUNKS
+HELD = 2
 NT = (((1,), (1,)), ((), ()))
 NN = (((1,), (0,)), ((), ()))
 
@@ -26,13 +28,14 @@
 
 
 def kernel(
-    far_mask, far_ids, far_count, near_ids, near_count,
+    far_mask_in, far_ids_in, far_count_in, near_ids_in, near_count_in,
     vectors, basis, leaf_transfer, upper_transfer, upper_coupling, leaf_coupling, near_blocks,
     out,
+    far_mask, far_ids, far_count, near_ids, near_count,
     near_w, coup_w, basis_w, trans_w, up_t, up_c,
     va, vb, cpa, cpb, dl, dr, near_acc, field,
     l0, l1, l2, l3, l4, cc,
-    sem_near, sem_in,
+    sem_near, sem_in, sem_small,
     v_send, v_recv, c_send, c_recv, p_send, p_recv, z_send, z_recv, e_send, e_recv,
 ):
     b = lax.axis_index("branch")
@@ -65,16 +68,25 @@
     load_trans[0] = local(leaf_transfer.at[0], trans_w.at[0], sem_in.at[2])
     load_ut = local(upper_transfer, up_t, sem_in.at[3])
     load_uc = local(upper_coupling, up_c, sem_in.at[4])
-    step = LEAF_DEV // CHUNKS
+    load_small = [
+        local(far_mask_in, far_mask, sem_small.at[0]),
+        local(far_ids_in, far_ids, sem_small.at[1]),
+        local(far_count_in, far_count, sem_small.at[2]),
+        local(near_ids_in, near_ids, sem_small.at[3]),
+        local(near_count_in, near_count, sem_small.at[4]),
+    ]
     for m in range(2):
         if m == 1:
             load_basis[1] = local(basis.at[1], basis_w.at[1], sem_in.at[5])
             load_trans[1] = local(leaf_transfer.at[1], trans_w.at[1], sem_in.at[6])
-        for g in range(CHUNKS):
-            part = pl.ds(g * step, step)
-            load_near[m].append(local(near_blocks.at[m, part], near_w.at[m, part], sem_near.at[m, g]))
-            if g == 1:
-                load_coup[m] = local(leaf_coupling.at[m], coup_w.at[m], sem_in.at[7 + m])
+        for g in range(2):
+            part = pl.ds(g * 16, 16)
+            load_near[m].append(local(near_blocks.at[m, part, 0], near_w.at[m, part, 0], sem_near.at[m, g]))
+        load_coup[m] = local(leaf_coupling.at[m], coup_w.at[m], sem_in.at[7 + m])
+        for g in range(6):
+            part = pl.ds((g % 2) * 16, 16)
+            slot = 1 + g // 2
+            load_near[m].append(local(near_blocks.at[m, part, slot], near_w.at[m, part, slot], sem_near.at[m, 2 + g]))
 
     barrier = pltpu.get_barrier_semaphore()
 
@@ -177,6 +189,40 @@
         dead = lax.shift_right_arithmetic(q - count, 31) + 1
         return (leaf - first_leaf) + dead * (96 - (leaf - first_leaf))
 
+    def far_rows(i):
+        count = far_count[i]
+
+        def spot(q):
+            return live_or_zero(q, count, far_ids[q, i])
+
+        return jnp.concatenate([dl[spot(2 * t)] + dr[spot(2 * t + 1)] for t in range(4)], axis=1)
+
+    def near_rest(m, source, i):
+        total = near_acc[:, pl.ds(pl.multiple_of(i * LEAF, LEAF), LEAF)]
+        count = near_count[i]
+        for q in range(1, 4):
+            piece = source[live_or_zero(q, count, near_ids[q, i])]
+            total = total + dot_nt(piece, near_w[m, i, q])
+        return total
+
+    def far_terms(m, p):
+        pair = field[:, pl.ds(pl.multiple_of(p * 128, 128), 128)]
+        none = jnp.zeros_like(pair)
+        lhs = jnp.concatenate([jnp.where(left, pair, none), jnp.where(left, none, pair)], axis=0).astype(jnp.bfloat16)
+        rhs = basis_w[m, pl.ds(2 * p, 2)].reshape(128, LEAF)
+        both = dot_nn(lhs, rhs)
+        return both[:COLS], both[COLS:]
+
+    def start_chunk(g):
+        copies = halo_sends(
+            1,
+            vb.at[pl.ds(LEAF_DEV + g * STEP, STEP)],
+            vb.at[pl.ds(g * STEP, STEP)],
+            vb.at[pl.ds(2 * LEAF_DEV + g * STEP, STEP)],
+            v_send, v_recv,
+        )
+        halo_start(copies)
+
     for m in range(2):
         source = va if m == 0 else vb
         cp = cpa if m == 0 else cpb
@@ -188,7 +234,7 @@
                 coef_pair(0, va, cpa, p)
                 return carry
 
-            lax.fori_loop(0, LEAF_DEV // 2, coef_body, 0, unroll=2)
+            lax.fori_loop(0, LEAF_DEV // 2, coef_body, 0, unroll=4)
         load_trans[m].wait()
         box = dot_nt(cp[:, pl.ds(LEAF_DEV * RANK, LEAF_DEV * RANK)], trans_w[m])
         l0[m, 3 + j] = masked_half(jnp.concatenate([box, box], axis=1), core)
@@ -208,9 +254,15 @@
         vec_halo = halo_sends(
             m, source.at[own], source.at[pl.ds(0, LEAF_DEV)], source.at[pl.ds(2 * LEAF_DEV, LEAF_DEV)], v_send, v_recv
         )
-        halo_start(vec_halo)
-
         if m == 0:
+            halo_start(vec_halo)
+        else:
+            for g in range(CHUNKS - HELD, CHUNKS):
+                start_chunk(g)
+
+        if m == 0:
+            for copy in load_small:
+                copy.wait()
             load_ut.wait()
             load_uc.wait()
             for mm in range(2):
@@ -221,15 +273,14 @@
                         blocks += [one, one]
                     cc[mm, h] = jnp.concatenate(blocks, axis=1)
 
-        for g in range(CHUNKS):
-            load_near[m][g].wait()
+        for copy in load_near[m][:2]:
+            copy.wait()
 
         def own_body(i, carry):
-            piece = source[LEAF_DEV + i]
-            near_acc[:, pl.ds(pl.multiple_of(i * LEAF, LEAF), LEAF)] = dot_nt(piece, near_w[m, i, 0])
+            near_acc[:, pl.ds(pl.multiple_of(i * LEAF, LEAF), LEAF)] = dot_nt(source[LEAF_DEV + i], near_w[m, i, 0])
             return carry
 
-        lax.fori_loop(0, LEAF_DEV, own_body, 0, unroll=2)
+        lax.fori_loop(0, LEAF_DEV, own_body, 0, unroll=8)
 
         for copy in plane:
             copy.wait_recv()
@@ -249,11 +300,12 @@
             l2[m, 4 + i] = n2[i]
         l3[m, z] = masked_half(lift(n2[0] + n2[1], 2), lax.rem(z, 2))
 
-        across = []
+        across = [None]
         for d in range(1, PLANES):
-            copy = remote(l3.at[m, z], l3.at[m, z], z_send.at[m, d], z_recv.at[m, d], z_peer[d])
-            copy.start()
-            across.append(copy)
+            across.append(remote(l3.at[m, z], l3.at[m, z], z_send.at[m, d], z_recv.at[m, d], z_peer[d]))
+        for d in (4, 3, 5, 2, 6, 1, 7):
+            across[d].start()
+        across = across[1:]
         up_one = b + PLANE
         down_one = b - PLANE
         up_two = b + 2 * PLANE
@@ -301,16 +353,8 @@
                 put_halves(2 * spot, pair)
             return carry
 
-        lax.fori_loop(0, LEAF_DEV // 2, dup_body, 0)
+        lax.fori_loop(0, LEAF_DEV // 2, dup_body, 0, unroll=4)
         load_coup[m].wait()
-
-        def far_rows(i):
-            count = far_count[i]
-
-            def spot(q):
-                return live_or_zero(q, count, far_ids[q, i])
-
-            return jnp.concatenate([dl[spot(2 * t)] + dr[spot(2 * t + 1)] for t in range(4)], axis=1)
 
         def coup_body(p, carry):
             lhs = jnp.concatenate([far_rows(2 * p), far_rows(2 * p + 1)], axis=0)
@@ -319,25 +363,18 @@
             field[:, pl.ds(pl.multiple_of(p * 128, 128), 128)] = jnp.where(left, both[:COLS], both[COLS:])
             return carry
 
-        lax.fori_loop(0, LEAF_DEV // 2, coup_body, 0, unroll=1)
-
-        halo_recv(vec_halo)
-
-        def near_body(i, carry):
-            where_to = pl.ds(pl.multiple_of(i * LEAF, LEAF), LEAF)
-            total = near_acc[:, where_to]
-            count = near_count[i]
-            for q in range(1, 4):
-                spot = live_or_zero(q, count, near_ids[q, i])
-                piece = source[spot]
-                total = total + dot_nt(piece, near_w[m, i, q])
-            near_acc[:, where_to] = total
-            return carry
-
-        lax.fori_loop(0, LEAF_DEV, near_body, 0, unroll=2)
-
-        for copy in across:
-            copy.wait_recv()
+        lax.fori_loop(0, LEAF_DEV // 2, coup_body, 0, unroll=4)
+
+        for copy in load_near[m][2:]:
+            copy.wait()
+        if m == 1:
+            halo_recv(vec_halo)
+
+            def near_body(i, carry):
+                near_acc[:, pl.ds(pl.multiple_of(i * LEAF, LEAF), LEAF)] = near_rest(m, source, i)
+                return carry
+
+            lax.fori_loop(0, LEAF_DEV, near_body, 0, unroll=4)
 
         @pl.when(z + 1 < PLANES)
         def _():
@@ -356,11 +393,6 @@
         @pl.when(z > 1)
         def _():
             up2.wait_recv()
-
-        pairs = jnp.concatenate([l3[m, 2 * i] + l3[m, 2 * i + 1] for i in range(4)], axis=0)
-        lifted = lift(pairs, 3)
-        for i in range(4):
-            l4[i] = masked_half(lifted[i * COLS:(i + 1) * COLS], 0)
 
         def node(h, o):
             if h == 0:
@@ -382,35 +414,58 @@
                 blocks.append(jnp.where(there, node(h, o), jnp.zeros((COLS, 128), jnp.bfloat16)) * live)
             return dot_nt(jnp.concatenate(blocks, axis=1), cc[m, h])
 
+        terms = [coupled(h) for h in range(3)]
+
+        for copy in across:
+            copy.wait_recv()
+
+        terms.append(coupled(3))
+        pairs = jnp.concatenate([l3[m, 2 * i] + l3[m, 2 * i + 1] for i in range(4)], axis=0)
+        lifted = lift(pairs, 3)
+        for i in range(4):
+            l4[i] = masked_half(lifted[i * COLS:(i + 1) * COLS], 0)
         descent = coupled(4)
         for h in (3, 2, 1, 0):
             both = dot_nn(descent.astype(jnp.bfloat16), up_t[m, h])
             side = lax.rem(b // (1 << h), 2)
-            descent = coupled(h) + jnp.where(side == 0, both[:, :RANK], both[:, RANK:])
+            descent = terms[h] + jnp.where(side == 0, both[:, :RANK], both[:, RANK:])
         parent = descent.astype(jnp.bfloat16)
         field[...] += dot_nn(parent, trans_w[m])
 
-        def final_body(p, carry):
-            pair = field[:, pl.ds(pl.multiple_of(p * 128, 128), 128)]
-            none = jnp.zeros_like(pair)
-            lhs = jnp.concatenate([jnp.where(left, pair, none), jnp.where(left, none, pair)], axis=0).astype(jnp.bfloat16)
-            rhs = basis_w[m, pl.ds(2 * p, 2)].reshape(128, LEAF)
-            both = dot_nn(lhs, rhs)
-            total = near_acc[:, pl.ds(pl.multiple_of(p * 512, 512), 512)]
-            first = (total[:, :LEAF] + both[:COLS]).astype(jnp.bfloat16)
-            second = (total[:, LEAF:] + both[COLS:]).astype(jnp.bfloat16)
-            if m == 0:
-                vb[LEAF_DEV + 2 * p] = first
-                vb[LEAF_DEV + 2 * p + 1] = second
-                coef_pair(1, vb, cpb, p)
-            else:
-                out[:, pl.ds(pl.multiple_of(p * 512, 512), LEAF)] = first
-                out[:, pl.ds(pl.multiple_of(p * 512 + LEAF, LEAF), LEAF)] = second
-            return carry
-
         if m == 0:
             load_basis[1].wait()
-        lax.fori_loop(0, LEAF_DEV // 2, final_body, 0, unroll=2)
+            halo_recv(vec_halo)
+
+            def join_body(g, carry):
+                before = g - (g + CHUNKS - 1) // CHUNKS
+                for k in range(STEP // 2):
+                    coef_pair(1, vb, cpb, before * (STEP // 2) + k)
+                for k in range(STEP // 2):
+                    p = g * (STEP // 2) + k
+                    far = far_terms(0, p)
+                    for s in range(2):
+                        vb[LEAF_DEV + 2 * p + s] = (near_rest(0, va, 2 * p + s) + far[s]).astype(jnp.bfloat16)
+
+                @pl.when(jnp.logical_and(g > 0, g <= CHUNKS - HELD))
+                def _():
+                    start_chunk(g - 1)
+
+                return carry
+
+            lax.fori_loop(0, CHUNKS, join_body, 0)
+            for k in range(STEP // 2):
+                coef_pair(1, vb, cpb, LEAF_DEV // 2 - STEP // 2 + k)
+        else:
+
+            def final_body(p, carry):
+                far = far_terms(1, p)
+                total = near_acc[:, pl.ds(pl.multiple_of(p * 512, 512), 512)]
+                for s in range(2):
+                    where_to = pl.ds(pl.multiple_of(p * 512 + s * LEAF, LEAF), LEAF)
+                    out[:, where_to] = (total[:, s * LEAF:(s + 1) * LEAF] + far[s]).astype(jnp.bfloat16)
+                return carry
+
+            lax.fori_loop(0, LEAF_DEV // 2, final_body, 0, unroll=4)
 
         for copy in plane + across:
             copy.wait_send()
@@ -440,17 +495,19 @@
     vectors, basis, leaf_transfer, upper_transfer, upper_coupling, leaf_coupling, near_blocks,
     far_mask, far_ids, far_count, near_ids, near_count,
 ):
-    smem = pl.BlockSpec(memory_space=pltpu.SMEM)
-    hbm = pl.BlockSpec(memory_space=pl.ANY)
+    smem = pltpu.SMEM
+    i32 = jnp.int32
+    hbm = pl.BlockSpec(memory_space=pltpu.HBM)
     bf = jnp.bfloat16
     f32 = jnp.float32
     dma = pltpu.SemaphoreType.DMA
     return pl.pallas_call(
         kernel,
         out_shape=jax.ShapeDtypeStruct((COLS, LEAF_DEV * LEAF), bf),
-        in_specs=[smem] * 5 + [hbm] * 7,
+        in_specs=[hbm] * 12,
         out_specs=pl.BlockSpec(memory_space=pltpu.VMEM),
         scratch_shapes=[
+            smem((5, 4, 64), i32), smem((8, LEAF_DEV), i32), smem((LEAF_DEV,), i32), smem((4, LEAF_DEV), i32), smem((LEAF_DEV,), i32),
             pltpu.VMEM((2, LEAF_DEV, 4, LEAF, LEAF), bf),
             pltpu.VMEM((2, LEAF_DEV, RANK, 512), bf),
             pltpu.VMEM((2, LEAF_DEV, RANK, LEAF), bf),
@@ -471,17 +528,22 @@
             pltpu.VMEM((2, 8, COLS, 128), bf),
             pltpu.VMEM((4, COLS, 128), bf),
             pltpu.VMEM((2, 5, RANK, 512), bf),
-            dma((2, CHUNKS)), dma((9,)),
+            dma((2, CHUNKS)), dma((9,)), dma((5,)),
             dma((2, 2)), dma((2, 2)), dma((2, 2)), dma((2, 2)),
             dma((2, 8)), dma((2, 8)), dma((2, 8)), dma((2, 8)), dma((2, 8)), dma((2, 8)),
         ],
         compiler_params=pltpu.CompilerParams(
-            collective_id=0, has_side_effects=True, vmem_limit_bytes=60 << 20
+            collective_id=0, has_side_effects=True, vmem_limit_bytes=50 << 20
         ),
         name="product",
     )(
-        jnp.transpose(far_mask, (0, 2, 1)), far_ids.T, far_count, near_ids.T, near_count,
-        vectors, basis, leaf_transfer, upper_transfer, upper_coupling, leaf_coupling, near_blocks,
+        *(
+            pltpu.with_memory_space_constraint(array, pltpu.HBM)
+            for array in (
+                jnp.transpose(far_mask, (0, 2, 1)), far_ids.T, far_count, near_ids.T, near_count,
+                vectors, basis, leaf_transfer, upper_transfer, upper_coupling, leaf_coupling, near_blocks,
+            )
+        )
     )
 
 

time: 59.7 us -> 49.5 us (0.83)
  the two profiles are of different devices: /device:TPU:39 before, /device:TPU:1 now
where the time goes in v2:
time: 49.5 us; the launch traced here: 48.7 us
  Pallas kernels  47.9 us (97%)
  local copies, waits for them, and re-layouts  0.8 us (2%)
    pallas_call x1, Pallas kernels, shards(): pl.pallas_call(kernel, out_shape=jax.ShapeDtypeStruct((COLS, LEAF_DEV * L...  47.9 us

profile of v2, /device:TPU:1, one launch (start us, length us, event | category | flops | bytes accessed | tf_op | source)
XLA Modules:
  0.0 48.7 jit_solution(4908347263234545242)
XLA Ops:
  0.0 47.9 %product.1 = bf16[32,8192]{1,0:T(8,128)(2,1)S(1)} custom-call(s32[5,4,64]{2,1,0:T(4,128)} %bitcast.3, s32[8,32]{1,0:T(8,128)} %bitcast.4, s32[32]{0:T(128)} %far_count_in.1, s32[4,32]{1,0:T(4,128)} %bitcast.5, s32[32]{0:T(128)} %near_count_in.1, bf16[32,8192]{1,0:T(8,128)(2,1)} %vectors.1, bf16[2,32,64,256]{3,2,1,0:T(8,128)(2,1)} %basis.1, ...), custom_call_target="tpu_custom_call" | custom-call | tf_op jit(solution)/shard_map/product/pallas_call | solution.py:504
  47.9 0.8 %copy.14 = bf16[32,8192]{1,0:T(8,128)(2,1)} copy(bf16[32,8192]{1,0:T(8,128)(2,1)S(1)} %product.1) | data formatting | bytes 1048576

commit v3 on v2

--- a/solution.py
+++ b/solution.py
@@ -15,6 +15,8 @@
 CHUNKS = 8
 STEP = LEAF_DEV // CHUNKS
 HELD = 2
+EARLY = 4
+AHEAD = 4
 NT = (((1,), (1,)), ((), ()))
 NN = (((1,), (0,)), ((), ()))
 
@@ -75,7 +77,7 @@
         local(near_ids_in, near_ids, sem_small.at[3]),
         local(near_count_in, near_count, sem_small.at[4]),
     ]
-    for m in range(2):
+    def start_first(m):
         if m == 1:
             load_basis[1] = local(basis.at[1], basis_w.at[1], sem_in.at[5])
             load_trans[1] = local(leaf_transfer.at[1], trans_w.at[1], sem_in.at[6])
@@ -83,10 +85,14 @@
             part = pl.ds(g * 16, 16)
             load_near[m].append(local(near_blocks.at[m, part, 0], near_w.at[m, part, 0], sem_near.at[m, g]))
         load_coup[m] = local(leaf_coupling.at[m], coup_w.at[m], sem_in.at[7 + m])
+
+    def start_rest(m):
         for g in range(6):
             part = pl.ds((g % 2) * 16, 16)
             slot = 1 + g // 2
             load_near[m].append(local(near_blocks.at[m, part, slot], near_w.at[m, part, slot], sem_near.at[m, 2 + g]))
+
+    start_first(0)
 
     barrier = pltpu.get_barrier_semaphore()
 
@@ -135,6 +141,24 @@
             copies[0].start()
 
         @pl.when(has_left)
+        def _():
+            copies[1].start()
+
+    def near_copies(copies, early):
+        @pl.when(has_right if early else j < PLANE - 1)
+        def _():
+            copies[0].start()
+
+        @pl.when(has_left if early else j > 0)
+        def _():
+            copies[1].start()
+
+    def late_copies(copies):
+        @pl.when(jnp.logical_and(has_right, j == PLANE - 1))
+        def _():
+            copies[0].start()
+
+        @pl.when(jnp.logical_and(has_left, j == 0))
         def _():
             copies[1].start()
 
@@ -213,15 +237,18 @@
         both = dot_nn(lhs, rhs)
         return both[:COLS], both[COLS:]
 
-    def start_chunk(g):
-        copies = halo_sends(
-            1,
-            vb.at[pl.ds(LEAF_DEV + g * STEP, STEP)],
-            vb.at[pl.ds(g * STEP, STEP)],
-            vb.at[pl.ds(2 * LEAF_DEV + g * STEP, STEP)],
+    def chunk_copies(m, g):
+        source = va if m == 0 else vb
+        return halo_sends(
+            m,
+            source.at[pl.ds(LEAF_DEV + g * STEP, STEP)],
+            source.at[pl.ds(g * STEP, STEP)],
+            source.at[pl.ds(2 * LEAF_DEV + g * STEP, STEP)],
             v_send, v_recv,
         )
-        halo_start(copies)
+
+    def start_chunk(g):
+        halo_start(chunk_copies(1, g))
 
     for m in range(2):
         source = va if m == 0 else vb
@@ -255,7 +282,9 @@
             m, source.at[own], source.at[pl.ds(0, LEAF_DEV)], source.at[pl.ds(2 * LEAF_DEV, LEAF_DEV)], v_send, v_recv
         )
         if m == 0:
-            halo_start(vec_halo)
+            for g in range(CHUNKS):
+                near_copies(chunk_copies(0, g), g < EARLY)
+            start_rest(0)
         else:
             for g in range(CHUNKS - HELD, CHUNKS):
                 start_chunk(g)
@@ -345,6 +374,11 @@
         def _():
             down2.start()
 
+        if m == 0:
+            for g in range(EARLY, CHUNKS):
+                late_copies(chunk_copies(0, g))
+            start_first(1)
+            start_rest(1)
         halo_recv(coef_halo)
 
         def dup_body(p, carry):
@@ -367,14 +401,13 @@
 
         for copy in load_near[m][2:]:
             copy.wait()
-        if m == 1:
-            halo_recv(vec_halo)
-
-            def near_body(i, carry):
-                near_acc[:, pl.ds(pl.multiple_of(i * LEAF, LEAF), LEAF)] = near_rest(m, source, i)
-                return carry
-
-            lax.fori_loop(0, LEAF_DEV, near_body, 0, unroll=4)
+        halo_recv(vec_halo)
+
+        def near_body(i, carry):
+            near_acc[:, pl.ds(pl.multiple_of(i * LEAF, LEAF), LEAF)] = near_rest(m, source, i)
+            return carry
+
+        lax.fori_loop(0, AHEAD * STEP if m == 0 else LEAF_DEV, near_body, 0, unroll=4)
 
         @pl.when(z + 1 < PLANES)
         def _():
@@ -434,27 +467,43 @@
 
         if m == 0:
             load_basis[1].wait()
-            halo_recv(vec_halo)
-
-            def join_body(g, carry):
-                before = g - (g + CHUNKS - 1) // CHUNKS
+
+            def coef_chunk(g):
                 for k in range(STEP // 2):
-                    coef_pair(1, vb, cpb, before * (STEP // 2) + k)
+                    coef_pair(1, vb, cpb, g * (STEP // 2) + k)
+
+            def join(g, near):
                 for k in range(STEP // 2):
                     p = g * (STEP // 2) + k
                     far = far_terms(0, p)
                     for s in range(2):
-                        vb[LEAF_DEV + 2 * p + s] = (near_rest(0, va, 2 * p + s) + far[s]).astype(jnp.bfloat16)
-
-                @pl.when(jnp.logical_and(g > 0, g <= CHUNKS - HELD))
+                        i = 2 * p + s
+                        total = near_rest(0, va, i) if near else near_acc[:, pl.ds(pl.multiple_of(i * LEAF, LEAF), LEAF)]
+                        vb[LEAF_DEV + i] = (total + far[s]).astype(jnp.bfloat16)
+
+            def ready_body(g, carry):
+                coef_chunk(g - (g + CHUNKS - 1) // CHUNKS)
+                join(g, False)
+
+                @pl.when(g > 0)
                 def _():
                     start_chunk(g - 1)
 
                 return carry
 
-            lax.fori_loop(0, CHUNKS, join_body, 0)
-            for k in range(STEP // 2):
-                coef_pair(1, vb, cpb, LEAF_DEV // 2 - STEP // 2 + k)
+            def join_body(g, carry):
+                coef_chunk(AHEAD + g - 1)
+                join(AHEAD + g, True)
+
+                @pl.when(AHEAD + g <= CHUNKS - HELD)
+                def _():
+                    start_chunk(AHEAD + g - 1)
+
+                return carry
+
+            lax.fori_loop(0, AHEAD, ready_body, 0)
+            lax.fori_loop(0, CHUNKS - AHEAD, join_body, 0)
+            coef_chunk(CHUNKS - 1)
         else:
 
             def final_body(p, carry):

time: 49.5 us -> 46.8 us (0.945); the launches traced: 48.7 us -> 46.8 us
  Pallas kernels: 47.9 us -> 46 us
    pallas_call x1, Pallas kernels: 47.9 us -> 46 us  [shards(): pl.pallas_call(kernel, out_shape=jax.ShapeDtypeStruct((COLS, LEAF_DEV * L...]
where the time goes in v3:
time: 46.8 us
  Pallas kernels  46 us (98%)
  local copies, waits for them, and re-layouts  0.8 us (2%)
    pallas_call x1, Pallas kernels, shards(): pl.pallas_call(kernel, out_shape=jax.ShapeDtypeStruct((COLS, LEAF_DEV * L...  46 us

profile of v3, /device:TPU:1, one launch (start us, length us, event | category | flops | bytes accessed | tf_op | source)
XLA Modules:
  0.0 46.8 jit_solution(18121625711269705890)
XLA Ops:
  0.0 46.0 %product.1 = bf16[32,8192]{1,0:T(8,128)(2,1)S(1)} custom-call(s32[5,4,64]{2,1,0:T(4,128)} %bitcast.3, s32[8,32]{1,0:T(8,128)} %bitcast.4, s32[32]{0:T(128)} %far_count_in.1, s32[4,32]{1,0:T(4,128)} %bitcast.5, s32[32]{0:T(128)} %near_count_in.1, bf16[32,8192]{1,0:T(8,128)(2,1)} %vectors.1, bf16[2,32,64,256]{3,2,1,0:T(8,128)(2,1)} %basis.1, ...), custom_call_target="tpu_custom_call" | custom-call | tf_op jit(solution)/shard_map/product/pallas_call | solution.py:553
  46.0 0.8 %copy.14 = bf16[32,8192]{1,0:T(8,128)(2,1)} copy(bf16[32,8192]{1,0:T(8,128)(2,1)S(1)} %product.1) | data formatting | bytes 1048576

commit v4 on v3

--- a/solution.py
+++ b/solution.py
@@ -15,8 +15,8 @@
 CHUNKS = 8
 STEP = LEAF_DEV // CHUNKS
 HELD = 2
-EARLY = 4
-AHEAD = 4
+EARLY = 8
+AHEAD = 2
 NT = (((1,), (1,)), ((), ()))
 NN = (((1,), (0,)), ((), ()))
 
@@ -36,7 +36,7 @@
     far_mask, far_ids, far_count, near_ids, near_count,
     near_w, coup_w, basis_w, trans_w, up_t, up_c,
     va, vb, cpa, cpb, dl, dr, near_acc, field,
-    l0, l1, l2, l3, l4, cc,
+    l0, l1, l2, l3, l4, cc, down_w,
     sem_near, sem_in, sem_small,
     v_send, v_recv, c_send, c_recv, p_send, p_recv, z_send, z_recv, e_send, e_recv,
 ):
@@ -301,6 +301,11 @@
                         one = up_c[mm, h, :, q * RANK:(q + 1) * RANK]
                         blocks += [one, one]
                     cc[mm, h] = jnp.concatenate(blocks, axis=1)
+                chain = None
+                for h in range(4):
+                    half = jnp.where(lax.rem(b // (1 << h), 2) == 0, up_t[mm, h, :, :RANK], up_t[mm, h, :, RANK:])
+                    chain = half if chain is None else dot_nn(half, chain).astype(jnp.bfloat16)
+                    down_w[mm, h] = chain
 
         for copy in load_near[m][:2]:
             copy.wait()
@@ -397,7 +402,7 @@
             field[:, pl.ds(pl.multiple_of(p * 128, 128), 128)] = jnp.where(left, both[:COLS], both[COLS:])
             return carry
 
-        lax.fori_loop(0, LEAF_DEV // 2, coup_body, 0, unroll=4)
+        lax.fori_loop(0, LEAF_DEV // 2, coup_body, 0, unroll=8)
 
         for copy in load_near[m][2:]:
             copy.wait()
@@ -407,7 +412,7 @@
             near_acc[:, pl.ds(pl.multiple_of(i * LEAF, LEAF), LEAF)] = near_rest(m, source, i)
             return carry
 
-        lax.fori_loop(0, AHEAD * STEP if m == 0 else LEAF_DEV, near_body, 0, unroll=4)
+        lax.fori_loop(0, AHEAD * STEP if m == 0 else LEAF_DEV, near_body, 0, unroll=8)
 
         @pl.when(z + 1 < PLANES)
         def _():
@@ -447,21 +452,20 @@
                 blocks.append(jnp.where(there, node(h, o), jnp.zeros((COLS, 128), jnp.bfloat16)) * live)
             return dot_nt(jnp.concatenate(blocks, axis=1), cc[m, h])
 
-        terms = [coupled(h) for h in range(3)]
+        def brought(h, term):
+            return dot_nn(term.astype(jnp.bfloat16), down_w[m, h - 1])
+
+        descent = coupled(0) + brought(1, coupled(1)) + brought(2, coupled(2))
 
         for copy in across:
             copy.wait_recv()
 
-        terms.append(coupled(3))
+        descent = descent + brought(3, coupled(3))
         pairs = jnp.concatenate([l3[m, 2 * i] + l3[m, 2 * i + 1] for i in range(4)], axis=0)
         lifted = lift(pairs, 3)
         for i in range(4):
             l4[i] = masked_half(lifted[i * COLS:(i + 1) * COLS], 0)
-        descent = coupled(4)
-        for h in (3, 2, 1, 0):
-            both = dot_nn(descent.astype(jnp.bfloat16), up_t[m, h])
-            side = lax.rem(b // (1 << h), 2)
-            descent = terms[h] + jnp.where(side == 0, both[:, :RANK], both[:, RANK:])
+        descent = descent + brought(4, coupled(4))
         parent = descent.astype(jnp.bfloat16)
         field[...] += dot_nn(parent, trans_w[m])
 
@@ -577,6 +581,7 @@
             pltpu.VMEM((2, 8, COLS, 128), bf),
             pltpu.VMEM((4, COLS, 128), bf),
             pltpu.VMEM((2, 5, RANK, 512), bf),
+            pltpu.VMEM((2, 4, RANK, RANK), bf),
             dma((2, CHUNKS)), dma((9,)), dma((5,)),
             dma((2, 2)), dma((2, 2)), dma((2, 2)), dma((2, 2)),
             dma((2, 8)), dma((2, 8)), dma((2, 8)), dma((2, 8)), dma((2, 8)), dma((2, 8)),

time: 46.8 us -> 43.4 us (0.927); the launches traced: 46.8 us -> 42.8 us
  Pallas kernels: 46 us -> 42 us
    pallas_call x1, Pallas kernels: 46 us -> 42 us  [shards(): pl.pallas_call(kernel, out_shape=jax.ShapeDtypeStruct((COLS, LEAF_DEV * L...]
where the time goes in v4:
time: 43.4 us; the launch traced here: 42.8 us
  Pallas kernels  42 us (97%)
  local copies, waits for them, and re-layouts  0.8 us (2%)
    pallas_call x1, Pallas kernels, shards(): pl.pallas_call(kernel, out_shape=jax.ShapeDtypeStruct((COLS, LEAF_DEV * L...  42 us

profile of v4, /device:TPU:1, one launch (start us, length us, event | category | flops | bytes accessed | tf_op | source)
XLA Modules:
  0.0 42.8 jit_solution(877463353196602413)
XLA Ops:
  0.0 42.0 %product.1 = bf16[32,8192]{1,0:T(8,128)(2,1)S(1)} custom-call(s32[5,4,64]{2,1,0:T(4,128)} %bitcast.3, s32[8,32]{1,0:T(8,128)} %bitcast.4, s32[32]{0:T(128)} %far_count_in.1, s32[4,32]{1,0:T(4,128)} %bitcast.5, s32[32]{0:T(128)} %near_count_in.1, bf16[32,8192]{1,0:T(8,128)(2,1)} %vectors.1, bf16[2,32,64,256]{3,2,1,0:T(8,128)(2,1)} %basis.1, ...), custom_call_target="tpu_custom_call" | custom-call | tf_op jit(solution)/shard_map/product/pallas_call | solution.py:557
  42.0 0.8 %copy.14 = bf16[32,8192]{1,0:T(8,128)(2,1)} copy(bf16[32,8192]{1,0:T(8,128)(2,1)S(1)} %product.1) | data formatting | bytes 1048576

commit v5 on v4

--- a/solution.py
+++ b/solution.py
@@ -261,7 +261,7 @@
                 coef_pair(0, va, cpa, p)
                 return carry
 
-            lax.fori_loop(0, LEAF_DEV // 2, coef_body, 0, unroll=4)
+            lax.fori_loop(0, LEAF_DEV // 2, coef_body, 0, unroll=8)
         load_trans[m].wait()
         box = dot_nt(cp[:, pl.ds(LEAF_DEV * RANK, LEAF_DEV * RANK)], trans_w[m])
         l0[m, 3 + j] = masked_half(jnp.concatenate([box, box], axis=1), core)
@@ -314,7 +314,7 @@
             near_acc[:, pl.ds(pl.multiple_of(i * LEAF, LEAF), LEAF)] = dot_nt(source[LEAF_DEV + i], near_w[m, i, 0])
             return carry
 
-        lax.fori_loop(0, LEAF_DEV, own_body, 0, unroll=8)
+        lax.fori_loop(0, LEAF_DEV, own_body, 0, unroll=16)
 
         for copy in plane:
             copy.wait_recv()
@@ -392,7 +392,7 @@
                 put_halves(2 * spot, pair)
             return carry
 
-        lax.fori_loop(0, LEAF_DEV // 2, dup_body, 0, unroll=4)
+        lax.fori_loop(0, LEAF_DEV // 2, dup_body, 0, unroll=8)
         load_coup[m].wait()
 
         def coup_body(p, carry):
@@ -412,7 +412,7 @@
             near_acc[:, pl.ds(pl.multiple_of(i * LEAF, LEAF), LEAF)] = near_rest(m, source, i)
             return carry
 
-        lax.fori_loop(0, AHEAD * STEP if m == 0 else LEAF_DEV, near_body, 0, unroll=8)
+        lax.fori_loop(0, AHEAD * STEP if m == 0 else LEAF_DEV, near_body, 0, unroll=16 if m else 8)
 
         @pl.when(z + 1 < PLANES)
         def _():
@@ -518,7 +518,7 @@
                     out[:, where_to] = (total[:, s * LEAF:(s + 1) * LEAF] + far[s]).astype(jnp.bfloat16)
                 return carry
 
-            lax.fori_loop(0, LEAF_DEV // 2, final_body, 0, unroll=4)
+            lax.fori_loop(0, LEAF_DEV // 2, final_body, 0, unroll=8)
 
         for copy in plane + across:
             copy.wait_send()

time: 43.4 us -> 43 us (level); the launches traced: 42.8 us -> 42.9 us
  no operation moved by 1% of the time
where the time goes in v5:
time: 43 us; the launch traced here: 42.9 us
  Pallas kernels  42.1 us (98%)
  local copies, waits for them, and re-layouts  0.8 us (2%)
    pallas_call x1, Pallas kernels, shards(): pl.pallas_call(kernel, out_shape=jax.ShapeDtypeStruct((COLS, LEAF_DEV * L...  42.1 us

profile of v5, /device:TPU:1, one launch (start us, length us, event | category | flops | bytes accessed | tf_op | source)
XLA Modules:
  0.0 42.9 jit_solution(17222290614576979145)
XLA Ops:
  0.0 42.1 %product.1 = bf16[32,8192]{1,0:T(8,128)(2,1)S(1)} custom-call(s32[5,4,64]{2,1,0:T(4,128)} %bitcast.3, s32[8,32]{1,0:T(8,128)} %bitcast.4, s32[32]{0:T(128)} %far_count_in.1, s32[4,32]{1,0:T(4,128)} %bitcast.5, s32[32]{0:T(128)} %near_count_in.1, bf16[32,8192]{1,0:T(8,128)(2,1)} %vectors.1, bf16[2,32,64,256]{3,2,1,0:T(8,128)(2,1)} %basis.1, ...), custom_call_target="tpu_custom_call" | custom-call | tf_op jit(solution)/shard_map/product/pallas_call | solution.py:557
  42.1 0.8 %copy.14 = bf16[32,8192]{1,0:T(8,128)(2,1)} copy(bf16[32,8192]{1,0:T(8,128)(2,1)S(1)} %product.1) | data formatting | bytes 1048576
